TPU v7x, 32 devices: a whole 2x2x4 slice. The times are simulated.
32 devices in a mesh: row: 8 (over z, y), col: 4 (over x, core).
Axes of the slice: x: 2, y: 2, z: 4, core: 2. Of those that a mesh axis runs over, the one named last changes fastest.
Arguments:
- fields: float32 [1, 4, 256, 256, 256], P(None, None, 'row', 'col'), may hold values from -6 to 6
- cotangent: float32 [1, 4, 256, 256, 256], P(None, None, 'row', 'col'), may hold values from -6 to 6
- spec_weights: float32 [2, 4, 4, 16, 16, 16], replicated, may hold values from -96 to 96
- point_weights: float32 [4, 4], replicated, may hold values from -3 to 3
- bias: float32 [4], replicated, may hold values from -3 to 3
Outputs:
- grad_fields: float32 [1, 4, 256, 256, 256], P(None, None, 'row', 'col')
- grad_spectral: float32 [2, 4, 4, 16, 16, 16], replicated
All inputs are finite; a program needn't handle non-finite values.
Results may differ from a plain program's by a relative error of at most 0.00011.
Values sent between devices are 32-bit elements; how exact they have to be, the bound alone decides.
A program may use at most 128 MiB of HBM per device.

v0:
```python
import functools
import math

import jax
import jax.numpy as jnp
import numpy as np
from jax import lax
from jax.experimental import pallas as pl
from jax.experimental.pallas import tpu as pltpu
from jax.sharding import PartitionSpec as P

f32 = jnp.float32
bf16 = jnp.bfloat16
MESH = pl.DeviceIdType.MESH
TILE = 256


def split(value):
    high = value.astype(bf16)
    return high, (value - high.astype(f32)).astype(bf16)


def split_np(value):
    value = np.asarray(value, np.float32)
    high = value.astype(jnp.bfloat16)
    low = (value - high.astype(np.float32)).astype(jnp.bfloat16)
    return high, low


def signed(number):
    wave = np.arange(number)
    return np.where(wave < number // 2, wave, wave - number)


def x_tables(chans, length, modes, cells):
    angle = 2.0 * np.pi / length * ((np.arange(length)[:, None] * np.arange(modes)) % length)
    first = np.concatenate([np.cos(angle), -np.sin(angle)], 1)
    weight = np.where(np.arange(modes) == 0, 1.0, 2.0) / cells
    last = np.concatenate([np.cos(angle) * weight, -np.sin(angle) * weight], 1).T
    eye = np.eye(chans)
    wide = (eye[:, None, :, None] * first[None, :, None, :]).reshape(chans * length, -1)
    high, low = split_np(wide)
    analysis = np.concatenate([high, low], 1)
    analysis = np.concatenate([analysis, analysis], 0)
    tall = (eye[:, None, :, None] * last[None, :, None, :]).reshape(-1, chans * length)
    high, low = split_np(tall)
    return analysis, np.concatenate([high, high, low], 0)


def yz_tables(ny, nz, my, mz):
    ang_y = 2.0 * np.pi / ny * ((np.arange(ny)[:, None] * signed(my)) % ny)
    ang_z = 2.0 * np.pi / nz * ((np.arange(nz)[:, None] * signed(mz)) % nz)
    tab_y = np.concatenate([np.repeat(np.cos(ang_y), mz, 1), np.repeat(np.sin(ang_y), mz, 1)], 1)
    tab_z = np.concatenate([np.tile(np.cos(ang_z), (1, my)), np.tile(np.sin(ang_z), (1, my))], 1)
    return tab_y.astype(np.float32), tab_z.astype(np.float32)


def dot(a, b):
    return jnp.dot(a, b, preferred_element_type=f32)


def dot_nt(a, b):
    return lax.dot_general(a, b, (((1,), (1,)), ((), ())), preferred_element_type=f32)


def analyse(split_x, w_ref, t_ref, acc):
    pairs = dot(split_x[...], w_ref[...])
    half = pairs.shape[1] // 2
    along_x = (pairs[:, :half] + pairs[:, half:]).T
    total = dot(jnp.concatenate(split(along_x), 0), t_ref[...])
    rows, lanes = total.shape[0] // 2, total.shape[1] // 2
    total = total[:rows] + total[rows:]
    part = total[:, :lanes] + total[:, lanes:]
    first = pl.program_id(0) == 0

    @pl.when(first)
    def _():
        acc[...] = part

    @pl.when(jnp.logical_not(first))
    def _():
        acc[...] = acc[...] + part


def modes_out(acc, out_ref, chans, modes):
    rows = acc.shape[0]
    lanes = acc.shape[1] // 2
    cosine, sine = acc[:, :lanes], acc[:, lanes:]
    halves = lanes // 128
    for c in range(chans):
        a, b, d = 2 * c * modes, (2 * c + 1) * modes, (2 * c + 2) * modes
        real = cosine[a:b] + sine[b:d]
        imag = cosine[b:d] - sine[a:b]
        for h in range(halves):
            out_ref[h * rows + a : h * rows + b] = real[:, h * 128 : (h + 1) * 128]
            out_ref[h * rows + b : h * rows + d] = imag[:, h * 128 : (h + 1) * 128]


def read_modes(ref, c, h, modes, rows):
    at = h * rows + 2 * c * modes
    return ref[at : at + modes], ref[at + modes : at + 2 * modes]


def put_modes(r_ref, c, h, modes, rows, lanes, real, imag):
    for at, value in ((0, real), (lanes, -imag)):
        for r, part in zip((0, rows), split(value)):
            r_ref[r + 2 * c * modes : r + (2 * c + 1) * modes, at + h * 128 : at + (h + 1) * 128] = part
    for at, value in ((0, imag), (lanes, real)):
        for r, part in zip((0, rows), split(value)):
            r_ref[r + (2 * c + 1) * modes : r + (2 * c + 2) * modes, at + h * 128 : at + (h + 1) * 128] = part


def synthesise(t_ref, r_ref, l_ref, spec):
    k = r_ref.shape[1]
    pairs = dot_nt(t_ref[:, :k], r_ref[...]) + dot_nt(t_ref[:, k:], r_ref[...])
    half = pairs.shape[1] // 2
    high, low = split(pairs[:, :half] + pairs[:, half:])
    spec[...] = dot(jnp.concatenate([high, low, high], 1), l_ref[...])


def kernel_a(dims, f_ref, w_ref, ty_ref, tz_ref, t_ref, u_ref, split_x, acc):
    chans, modes, ylines, zlines, ty, nx = dims
    j = pl.program_id(0)
    lanes = ty_ref.shape[1] // 2

    y0 = lax.axis_index("row") * ylines + j * ty
    z0 = pl.multiple_of(lax.axis_index("col") * zlines, zlines)

    def table(k, carry):
        ys = ty_ref[pl.ds(y0 + k, 1), :]
        zs = tz_ref[pl.ds(z0, zlines), :]
        yc, yn = ys[:, :lanes], ys[:, lanes:]
        zc, zn = zs[:, :lanes], zs[:, lanes:]
        rows = pl.ds(pl.multiple_of(k * zlines, zlines), zlines)
        for at, value in ((0, yc * zc - yn * zn), (lanes, yn * zc + yc * zn)):
            high, low = split(value)
            t_ref[rows, at : at + lanes] = high
            t_ref[rows, 2 * lanes + at : 2 * lanes + at + lanes] = low
        return carry

    lax.fori_loop(0, ty, table, 0)

    def cut(k, carry):
        rows = pl.ds(pl.multiple_of(k * zlines, zlines), zlines)
        for c in range(chans):
            high, low = split(f_ref[0, c, k])
            split_x[rows, c * nx : (c + 1) * nx] = high
            split_x[rows, (chans + c) * nx : (chans + c + 1) * nx] = low
        return carry

    lax.fori_loop(0, ty, cut, 0)
    analyse(split_x, w_ref, t_ref, acc)

    @pl.when(j == pl.num_programs(0) - 1)
    def _():
        modes_out(acc, u_ref, chans, modes)


ERFC = (0.254829592, -0.284496736, 1.421413741, -1.453152027, 1.061405429)


def gelu_slope(v):
    a = jnp.abs(v)
    t = pl.reciprocal(1.0 + (0.3275911 / math.sqrt(2.0)) * a, approx=False)
    poly = 0.5 * ERFC[4]
    for coef in ERFC[3::-1]:
        poly = poly * t + 0.5 * coef
    gauss = jnp.exp2(v * v * (-0.5 / math.log(2.0)))
    tail = gauss * (poly * t - a * (1.0 / math.sqrt(2.0 * math.pi)))
    return jnp.where(v < 0.0, tail, 1.0 - tail)


def kernel_b(dims, u_ref, sw_ref, pw_ref, b_ref, f_ref, g_ref, w_ref, l_ref, t_ref,
             h_ref, s_ref, r_ref, spec, split_x, acc):
    chans, modes, ylines, zlines, ty, nx = dims
    j = pl.program_id(0)
    lanes = t_ref.shape[1] // 4
    rows_m = acc.shape[0]

    @pl.when(j == 0)
    def _():
        for h in range(lanes // 128):
            at = slice(h * 128, (h + 1) * 128)
            for o in range(chans):
                real = imag = 0.0
                for i in range(chans):
                    ur, ui = read_modes(u_ref, i, h, modes, rows_m)
                    wr, wi = sw_ref[0, i, o, :, at], sw_ref[1, i, o, :, at]
                    real += ur * wr - ui * wi
                    imag += ur * wi + ui * wr
                put_modes(r_ref, o, h, modes, rows_m, lanes, real, imag)

    synthesise(t_ref, r_ref, l_ref, spec)
    step = 16
    per = zlines // step

    def cells(k, carry):
        y, z = k // per, k % per
        zs = pl.ds(pl.multiple_of(z * step, step), step)
        rows = pl.ds(pl.multiple_of(k * step, step), step)
        fields = [f_ref[0, i, y, zs, :] for i in range(chans)]
        for o in range(chans):
            pre = spec[rows, o * nx : (o + 1) * nx] + b_ref[o]
            for i in range(chans):
                pre += fields[i] * pw_ref[i, o]
            up = g_ref[0, o, y, zs, :] * gelu_slope(pre)
            h_ref[0, o, y, zs, :] = up
            high, low = split(up)
            split_x[rows, o * nx : (o + 1) * nx] = high
            split_x[rows, (chans + o) * nx : (chans + o + 1) * nx] = low
        return carry

    lax.fori_loop(0, ty * per, cells, 0)
    analyse(split_x, w_ref, t_ref, acc)

    @pl.when(j == pl.num_programs(0) - 1)
    def _():
        modes_out(acc, s_ref, chans, modes)


def kernel_c(dims, cells_all, u_ref, s_ref, sw_ref, pw_ref, h_ref, l_ref, t_ref,
             o_ref, gs_ref, r_ref, spec):
    chans, modes, ylines, zlines, ty, nx = dims
    j = pl.program_id(0)
    lanes = t_ref.shape[1] // 4
    rows_m = r_ref.shape[0] // 2

    @pl.when(j == 0)
    def _():
        wave = lax.broadcasted_iota(jnp.int32, (modes, 128), 0)
        factor = jnp.where(wave == 0, 1.0 / cells_all, 2.0 / cells_all).astype(f32)
        for h in range(lanes // 128):
            at = slice(h * 128, (h + 1) * 128)
            for i in range(chans):
                ur, ui = read_modes(u_ref, i, h, modes, rows_m)
                ur, ui = ur * factor, ui * factor
                real = imag = 0.0
                for o in range(chans):
                    hr, hi = read_modes(s_ref, o, h, modes, rows_m)
                    wr, wi = sw_ref[0, i, o, :, at], sw_ref[1, i, o, :, at]
                    gs_ref[0, i, o, :, at] = ur * hr + ui * hi
                    gs_ref[1, i, o, :, at] = ur * hi - ui * hr
                    real += wr * hr + wi * hi
                    imag += wr * hi - wi * hr
                put_modes(r_ref, i, h, modes, rows_m, lanes, real, imag)

    synthesise(t_ref, r_ref, l_ref, spec)
    step = 16
    per = zlines // step

    def cells(k, carry):
        y, z = k // per, k % per
        zs = pl.ds(pl.multiple_of(z * step, step), step)
        rows = pl.ds(pl.multiple_of(k * step, step), step)
        ups = [h_ref[0, o, y, zs, :] for o in range(chans)]
        for i in range(chans):
            out = spec[rows, i * nx : (i + 1) * nx]
            for o in range(chans):
                out += ups[o] * pw_ref[i, o]
            o_ref[0, i, y, zs, :] = out
        return carry

    lax.fori_loop(0, ty * per, cells, 0)


def sum_kernel(count, cols, x_ref, o_ref, got, gathered, send_a, recv_a, send_b, recv_b):
    me = lax.axis_index("row") * cols + lax.axis_index("col")

    def other(k):
        t = lax.rem(me + k, count)
        return t, {"row": t // cols, "col": lax.rem(t, cols)}

    barrier = pltpu.get_barrier_semaphore()

    def greet(k, carry):
        pl.semaphore_signal(barrier, inc=1, device_id=other(k)[1], device_id_type=MESH)
        return carry

    lax.fori_loop(1, count, greet, 0)
    pl.semaphore_wait(barrier, count - 1)

    def part(k, arriving):
        t, dev = other(k)
        slot = t if arriving else me
        return pltpu.make_async_remote_copy(
            src_ref=x_ref.at[t], dst_ref=got.at[slot], send_sem=send_a.at[t],
            recv_sem=recv_a.at[slot], device_id=dev, device_id_type=MESH)

    def whole(k, arriving):
        t, dev = other(k)
        slot = t if arriving else me
        return pltpu.make_async_remote_copy(
            src_ref=gathered.at[me], dst_ref=gathered.at[slot], send_sem=send_b.at[t],
            recv_sem=recv_b.at[slot], device_id=dev, device_id_type=MESH)

    def each(action):
        def body(k, carry):
            action(k)
            return carry
        lax.fori_loop(1, count, body, 0)

    each(lambda k: part(k, False).start())
    got[pl.ds(me, 1)] = x_ref[pl.ds(me, 1)]
    each(lambda k: part(k, True).wait_recv())
    gathered[pl.ds(me, 1)] = jnp.sum(got[...], axis=0, keepdims=True)
    each(lambda k: whole(k, False).start())
    each(lambda k: whole(k, True).wait_recv())
    o_ref[...] = gathered[...]
    each(lambda k: part(k, False).wait_send())
    each(lambda k: whole(k, False).wait_send())


def sum_modes(part, count, cols, ident):
    rows, lanes = part.shape
    shape = (count, rows // count, lanes)
    vmem = pl.BlockSpec(memory_space=pltpu.VMEM)
    out = pl.pallas_call(
        functools.partial(sum_kernel, count, cols),
        out_shape=jax.ShapeDtypeStruct(shape, f32),
        in_specs=[vmem],
        out_specs=vmem,
        scratch_shapes=[pltpu.VMEM(shape, f32), pltpu.VMEM(shape, f32)]
        + [pltpu.SemaphoreType.DMA((count,))] * 4,
        compiler_params=pltpu.CompilerParams(collective_id=ident, has_side_effects=True),
        name="sum_modes",
    )(part.reshape(shape))
    return out.reshape(rows, lanes)


def solution(mesh):
    nrow, ncol = mesh.shape["row"], mesh.shape["col"]
    count = nrow * ncol

    def per_device(fields, cotangent, spec_weights, point_weights, bias):
        _, chans, ylines, zlines, nx = fields.shape
        _, _, _, mx, my, mz = spec_weights.shape
        ny, nz = ylines * nrow, zlines * ncol
        cells_all = float(nx * ny * nz)
        lanes = my * mz
        rows_m = 2 * chans * mx
        ty = max(1, min(ylines, TILE // zlines))
        steps = ylines // ty
        tile = ty * zlines
        dims = (chans, mx, ylines, zlines, ty, nx)
        w_tab, l_tab = x_tables(chans, nx, mx, cells_all)
        y_tab, z_tab = yz_tables(ny, nz, my, mz)
        weights = spec_weights.reshape(2, chans, chans, mx, lanes)

        def keep(shape):
            return pl.BlockSpec(shape, lambda j: (0,) * len(shape))

        cells = pl.BlockSpec((1, chans, ty, zlines, nx), lambda j: (0, 0, j, 0, 0))
        table = pl.BlockSpec((tile, 4 * lanes), lambda j: (j, 0))
        smem = pl.BlockSpec(memory_space=pltpu.SMEM)
        field_shape = jax.ShapeDtypeStruct(fields.shape, f32)
        mode_shape = (rows_m * lanes // 128, 128)
        mode_out = jax.ShapeDtypeStruct(mode_shape, f32)
        x_scratch = pltpu.VMEM((tile, 2 * chans * nx), bf16)
        spec_scratch = pltpu.VMEM((tile, chans * nx), f32)
        acc_scratch = pltpu.VMEM((rows_m, 2 * lanes), f32)
        r_scratch = pltpu.VMEM((2 * rows_m, 2 * lanes), bf16)
        params = pltpu.CompilerParams(
            dimension_semantics=("arbitrary",), vmem_limit_bytes=56 * 1024 * 1024)

        t_tab, u_part = pl.pallas_call(
            functools.partial(kernel_a, dims),
            grid=(steps,),
            out_shape=(jax.ShapeDtypeStruct((ylines * zlines, 4 * lanes), bf16), mode_out),
            in_specs=[cells, keep(w_tab.shape), keep(y_tab.shape), keep(z_tab.shape)],
            out_specs=(table, keep(mode_shape)),
            scratch_shapes=[x_scratch, acc_scratch],
            compiler_params=params,
            name="analyse_fields",
        )(fields, w_tab, y_tab, z_tab)
        spectrum_u = sum_modes(u_part, count, ncol, 0)

        upstream, h_part = pl.pallas_call(
            functools.partial(kernel_b, dims),
            grid=(steps,),
            out_shape=(field_shape, mode_out),
            in_specs=[keep(mode_shape), keep(weights.shape), smem, smem, cells, cells,
                      keep(w_tab.shape), keep(l_tab.shape), table],
            out_specs=(cells, keep(mode_shape)),
            scratch_shapes=[r_scratch, spec_scratch, x_scratch, acc_scratch],
            compiler_params=params,
            name="layer_and_slope",
        )(spectrum_u, weights, point_weights, bias, fields, cotangent, w_tab, l_tab, t_tab)
        spectrum_h = sum_modes(h_part, count, ncol, 1)

        grad_fields, grad_spectral = pl.pallas_call(
            functools.partial(kernel_c, dims, cells_all),
            grid=(steps,),
            out_shape=(field_shape, jax.ShapeDtypeStruct(weights.shape, f32)),
            in_specs=[keep(mode_shape), keep(mode_shape), keep(weights.shape), smem, cells,
                      keep(l_tab.shape), table],
            out_specs=(cells, keep(weights.shape)),
            scratch_shapes=[r_scratch, spec_scratch],
            compiler_params=params,
            name="gradients",
        )(spectrum_u, spectrum_h, weights, point_weights, upstream, l_tab, t_tab)
        return grad_fields, grad_spectral.reshape(spec_weights.shape)

    placed = (P(None, None, "row", "col", None), P(None, None, "row", "col", None), P(), P(), P())
    return jax.shard_map(
        per_device,
        mesh=mesh,
        in_specs=placed,
        out_specs=(P(None, None, "row", "col", None), P()),
        check_vma=False,
    )
```

profile of v0, /device:TPU:0, one launch (start us, length us, event | category | flops | bytes accessed | tf_op | source)
XLA Modules:
  0.0 107.6 jit_solution(14811948801303992802)
XLA Ops:
  0.6 4.2 %reshape.24.sw_ref = f32[2,4,4,16,256]{4,3,2,1,0:T(8,128)} reshape(f32[2,4,4,16,16,16]{5,4,3,2,1,0:T(8,128)} %param.11) | data formatting | bytes 1048576 | tf_op jit(solution)/shard_map/reshape | solution.py:347
  4.8 13.4 %analyse_fields.1 = (bf16[2048,1024]{1,0:T(8,128)(2,1)}, f32[256,128]{1,0:T(8,128)}) custom-call(f32[1,4,32,64,256]{4,3,2,1,0:T(8,128)} %f_ref.3, bf16[2048,256]{1,0:T(8,128)(2,1)} %constant.8.clone.w_ref, f32[256,512]{1,0:T(8,128)} %constant.9.clone.ty_ref, f32[256,512]{1,0:T(8,128)} %constant.10.clone.tz_ref), custom_call_target="tpu_custom_call" | custom-call | tf_op jit(solution)/shard_map/analyse_fields/pallas_call | solution.py:365
  18.3 20.9 %sum_modes.2 = f32[32,8,128]{2,1,0:T(8,128)} custom-call(f32[32,8,128]{2,1,0:T(8,128)} %bitcast.11), custom_call_target="tpu_custom_call" | custom-call | tf_op jit(solution)/shard_map/sum_modes/pallas_call | solution.py:317
  39.2 32.3 %layer_and_slope.1 = (f32[1,4,32,64,256]{4,3,2,1,0:T(8,128)}, f32[256,128]{1,0:T(8,128)}) custom-call(f32[256,128]{1,0:T(8,128)} %bitcast.8, f32[2,4,4,16,256]{4,3,2,1,0:T(8,128)} %reshape.24.sw_ref, f32[4,4]{1,0:T(4,128)} %pw_ref.3, f32[4]{0:T(128)} %b_ref.1, f32[1,4,32,64,256]{4,3,2,1,0:T(8,128)} %f_ref.3, f32[1,4,32,64,256]{4,3,2,1,0:T(8,128)} %g_ref.1, ...), custom_call_target="tpu_custom_call" | custom-call | tf_op jit(solution)/shard_map/layer_and_slope/pallas_call | solution.py:377
  71.4 16.4 %sum_modes.3 = f32[32,8,128]{2,1,0:T(8,128)} custom-call(f32[32,8,128]{2,1,0:T(8,128)} %bitcast.12), custom_call_target="tpu_custom_call" | custom-call | tf_op jit(solution)/shard_map/sum_modes/pallas_call | solution.py:317
  87.9 16.1 %gradients.1 = (f32[1,4,32,64,256]{4,3,2,1,0:T(8,128)}, f32[2,4,4,16,256]{4,3,2,1,0:T(8,128)}) custom-call(f32[256,128]{1,0:T(8,128)} %bitcast.9, f32[256,128]{1,0:T(8,128)} %bitcast.10, f32[2,4,4,16,256]{4,3,2,1,0:T(8,128)} %reshape.24.sw_ref, f32[4,4]{1,0:T(4,128)} %pw_ref.3, f32[1,4,32,64,256]{4,3,2,1,0:T(8,128)} %get-tuple-element.11.h_ref, ...), custom_call_target="tpu_custom_call" | custom-call | tf_op jit(solution)/shard_map/gradients/pallas_call | solution.py:390
  104.0 3.7 %reshape.27 = f32[2,4,4,16,16,16]{5,4,3,2,1,0:T(8,128)} reshape(f32[2,4,4,16,256]{4,3,2,1,0:T(8,128)} %get-tuple-element.13) | data formatting | bytes 1048576 | tf_op jit(solution)/shard_map/reshape | solution.py:401
where the time goes:
time: 108 us
  Pallas kernels  99.1 us (92%)
  local copies, waits for them, and re-layouts  7.89 us (7%)
    pallas_call x2, Pallas kernels, sum_modes(): pl.pallas_call(functools.partial(sum_kernel, count, cols), out_shape=jax....  37.3 us
    pallas_call x1, Pallas kernels, per_device(): pl.pallas_call(functools.partial(kernel_b, dims), grid=(steps,), out_shap...  32.3 us
    pallas_call x1, Pallas kernels, per_device(): pl.pallas_call(functools.partial(kernel_c, dims, cells_all), grid=(steps,...  16.1 us
    pallas_call x1, Pallas kernels, per_device(): pl.pallas_call(functools.partial(kernel_a, dims), grid=(steps,), out_shap...  13.4 us
    reshape x1, local copies, waits for them, and re-layouts, per_device(): weights = spec_weights.reshape(2, chans, chans, mx, lanes)  4.21 us
    reshape x1, local copies, waits for them, and re-layouts, per_device(): return (grad_fields, grad_spectral.reshape(spec_weights.shape))  3.68 us

commit v1 on v0

v1 whole, which is shorter than its diff:
```python
import functools
import math

import jax
import jax.numpy as jnp
import numpy as np
from jax import lax
from jax.experimental import pallas as pl
from jax.experimental.pallas import tpu as pltpu
from jax.sharding import PartitionSpec as P

f32 = jnp.float32
bf16 = jnp.bfloat16
MESH = pl.DeviceIdType.MESH
TILE = 512
ROWS = 8
LANES = 128


def split(value):
    high = value.astype(bf16)
    return high, (value - high.astype(f32)).astype(bf16)


def split_np(value):
    value = np.asarray(value, np.float32)
    high = value.astype(jnp.bfloat16)
    low = (value - high.astype(np.float32)).astype(jnp.bfloat16)
    return high, low


def signed(number):
    wave = np.arange(number)
    return np.where(wave < number // 2, wave, wave - number)


def x_tables(chans, length, modes, cells):
    angle = 2.0 * np.pi / length * ((np.arange(length)[:, None] * np.arange(modes)) % length)
    weight = np.where(np.arange(modes) == 0, 1.0, 2.0) / cells
    eye = np.eye(chans)
    first = np.stack([np.cos(angle), -np.sin(angle)], 1)
    wide = np.einsum("cd,xkp->cxkdp", eye, first).reshape(chans * length, -1)
    tall = np.einsum("cd,xkp->kcpdx", eye, first * weight).reshape(-1, chans * length)
    return np.concatenate(split_np(wide), 1), np.concatenate(split_np(tall), 0)


def yz_tables(ny, nz, my, mz, ty, ylines, zlines, nrow, ncol):
    ky, kz = np.repeat(signed(my), mz), np.tile(signed(mz), my)

    def turns(y, z):
        return ((np.outer(y, ky) % ny) / ny + (np.outer(z, kz) % nz) / nz) * 2.0 * np.pi

    angle = turns(np.repeat(np.arange(ty), zlines), np.tile(np.arange(zlines), ty))
    high, low = split_np(np.concatenate([np.cos(angle), np.sin(angle)], 1))
    device_y = np.repeat(np.arange(nrow) * ylines, ncol)
    device_z = np.tile(np.arange(ncol) * zlines, nrow)
    start = turns(device_y, device_z).T
    end = turns(device_y + ylines - ty, device_z).T
    step = turns(np.array([ty]), np.array([0])).T
    phase = np.concatenate(
        [np.cos(start), np.sin(start), np.cos(end), np.sin(end), np.cos(step), np.sin(step)], 1)
    return (np.concatenate([high.T, low.T], 1), np.concatenate([high, low], 1),
            phase.astype(np.float32))


def dot(a, b):
    return jnp.dot(a, b, preferred_element_type=f32)


def lane_ids(rows):
    return lax.broadcasted_iota(jnp.int32, (rows, LANES), 1)


def times_i(value):
    turned = pltpu.roll(value, LANES // 2, 1)
    return jnp.where(lane_ids(value.shape[0]) < LANES // 2, -turned, turned)


def analyse(xs, wt_v, an_v, acc, step_cos, step_sin):
    pairs = dot(xs[...], wt_v[...])
    part = jnp.concatenate(split(pairs[:, :LANES] + pairs[:, LANES:]), 1)
    both = dot(an_v[...], jnp.concatenate([part, part], 0))
    both = both[:, :LANES] + both[:, LANES:]
    modes = both.shape[0] // 2
    c, s = acc[0], acc[1]
    new_c = c * step_cos[...] + s * step_sin[...] + both[:modes]
    new_s = s * step_cos[...] - c * step_sin[...] + both[modes:]
    acc[0] = new_c
    acc[1] = new_s


def spectrum(acc, end_cos, end_sin):
    c, s = acc[0], acc[1]
    cosine = c * end_cos[...] - s * end_sin[...]
    sine = s * end_cos[...] + c * end_sin[...]
    return cosine - times_i(sine)


def mode_rhs(turn, rhs):
    modes = turn.shape[1]
    for k in range(2):
        high, low = split(turn[k])
        rhs[k * modes : (k + 1) * modes, :LANES] = high
        rhs[k * modes : (k + 1) * modes, LANES:] = low


def turn_on(turn, step_cos, step_sin):
    m, im = turn[0], turn[1]
    turn[0] = m * step_cos[...] + im * step_sin[...]
    turn[1] = im * step_cos[...] - m * step_sin[...]


def synthesise(sy_v, rhs, l_v, spec):
    pairs = dot(sy_v[...], jnp.concatenate([rhs[...], rhs[...]], 0))
    high, low = split(pairs[:, :LANES] + pairs[:, LANES:])
    spec[...] = dot(jnp.concatenate([high, low, high, low], 1), l_v[...])


def gelu_slope(v):
    arg = v * math.sqrt(0.5)
    gauss = jnp.exp2(arg * arg * (-1.0 / math.log(2.0)))
    return (0.5 * lax.erf(arg) + 0.5) + (v * (1.0 / math.sqrt(2.0 * math.pi))) * gauss


def fill_twice(src, dst, sems, at):
    rows, out = src.shape[0], []
    for k in range(2):
        out.append(pltpu.make_async_copy(src, dst.at[pl.ds(k * rows, rows)], sems.at[at + k]))
    return out


def fill_synthesis(src, dst, sems, at):
    rows, out = src.shape[0] // 2, []
    for k in range(4):
        out.append(pltpu.make_async_copy(
            src.at[pl.ds(k // 2 * rows, rows)], dst.at[pl.ds(k * rows, rows)], sems.at[at + k]))
    return out


def layer_kernel(dims, f_hbm, g_hbm, w_hbm, pw, bias, wt_hbm, l_hbm, an_hbm, sy_hbm, ph_ref,
                 loc_hbm, a_ref, u_ref, h_ref,
                 f_v, g_v, loc_v, w_v, wown, wt_v, l_v, an_v, sy_v, xs, spec, acc, turn, rhs,
                 phase, part, got1, got2, mg, ug, ag, hg,
                 f_sem, g_sem, out_sem, tab_sem,
                 s1, r1, sm, rm, su, ru, s2, r2, sa, ra, sh, rh):
    chans, mx, my, mz, ylines, zlines, nx, ty, count, cols, owners = dims
    modes = my * mz
    steps = ylines // ty
    me = lax.axis_index("row") * cols + lax.axis_index("col")

    def device(t):
        return {"row": t // cols, "col": lax.rem(t, cols)}

    barrier = pltpu.get_barrier_semaphore()

    def greet(k, carry):
        pl.semaphore_signal(barrier, inc=1, device_id=device(lax.rem(me + k, count)), device_id_type=MESH)
        return carry

    lax.fori_loop(1, count, greet, 0)

    q = jnp.minimum(me, owners - 1) * ROWS // mz
    r0 = pl.multiple_of(lax.rem(jnp.minimum(me, owners - 1) * ROWS, mz), ROWS)
    q8 = pl.multiple_of(q // 8 * 8, 8)

    def tile_copy(src, dst, sem, j):
        rows = pl.ds(j * ty, ty)
        return pltpu.make_async_copy(src.at[0, :, rows], dst.at[:, rows], sem.at[j])

    wt_copies = fill_twice(wt_hbm, wt_v, tab_sem, 0)
    l_copies = fill_synthesis(l_hbm, l_v, tab_sem, 2)
    an_copy = pltpu.make_async_copy(an_hbm, an_v, tab_sem.at[6])
    sy_copy = pltpu.make_async_copy(sy_hbm, sy_v, tab_sem.at[7])
    w_copy = pltpu.make_async_copy(w_hbm.at[:, pl.ds(q8, 8), :], w_v, tab_sem.at[8])
    for copy in wt_copies:
        copy.start()
    tile_copy(f_hbm, f_v, f_sem, 0).start()
    an_copy.start()
    for j in range(1, steps):
        tile_copy(f_hbm, f_v, f_sem, j).start()
    w_copy.start()
    sy_copy.start()
    for copy in l_copies:
        copy.start()
    for j in range(steps):
        tile_copy(g_hbm, g_v, g_sem, j).start()

    place = lax.broadcasted_iota(jnp.int32, (modes, count), 1) == me
    for k in range(4):
        column = jnp.sum(jnp.where(place, ph_ref[:, k * count : (k + 1) * count], 0.0), axis=1, keepdims=True)
        phase[k] = jnp.broadcast_to(column, (modes, LANES))
    for k in range(2):
        phase[4 + k] = jnp.broadcast_to(ph_ref[:, 4 * count + k : 4 * count + k + 1], (modes, LANES))
    start_cos, start_sin, end_cos, end_sin, step_cos, step_sin = [phase.at[k] for k in range(6)]
    acc[...] = jnp.zeros_like(acc)

    for copy in wt_copies:
        copy.wait()
    an_copy.wait()

    def first(j, carry):
        tile_copy(f_hbm, f_v, f_sem, j).wait()

        def cut(k, carry):
            rows = pl.ds(pl.multiple_of(k * zlines, zlines), zlines)
            for c in range(chans):
                high, low = split(f_v[c, j * ty + k])
                xs[rows, c * nx : (c + 1) * nx] = high
                xs[rows, (chans + c) * nx : (chans + c + 1) * nx] = low
            return carry

        lax.fori_loop(0, ty, cut, 0)
        analyse(xs, wt_v, an_v, acc, step_cos, step_sin)
        return carry

    lax.fori_loop(0, steps, first, 0)
    part[0] = spectrum(acc, end_cos, end_sin).reshape(owners, ROWS, LANES)
    pl.semaphore_wait(barrier, count - 1)

    def piece(src, dst, send, recv, k, arriving, scatter):
        t = lax.rem(me + k, count)
        slot = t if arriving else me
        return pltpu.make_async_remote_copy(
            src_ref=src.at[t if scatter else me], dst_ref=dst.at[slot], send_sem=send.at[t],
            recv_sem=recv.at[slot], device_id=device(t), device_id_type=MESH)

    def each(action):
        def body(k, carry):
            action(k)
            return carry
        lax.fori_loop(1, count, body, 0)

    def owned(k, action):
        if owners == count:
            action()
        else:
            pl.when(lax.rem(me + k, count) < owners)(action)

    def owner(action):
        if owners == count:
            action()
        else:
            pl.when(me < owners)(action)

    def scatter_start(src, dst, send, recv):
        each(lambda k: owned(k, lambda: piece(src, dst, send, recv, k, False, True).start()))

    def scatter_sent(src, dst, send, recv):
        each(lambda k: owned(k, lambda: piece(src, dst, send, recv, k, False, True).wait_send()))

    def scatter_sum(src, dst, send, recv):
        each(lambda k: piece(src, dst, send, recv, k, True, False).wait_recv())
        dst[pl.ds(me, 1)] = src[pl.ds(me, 1)]
        return jnp.sum(dst[...], axis=0)

    def gather_start(ref, send, recv):
        each(lambda k: piece(ref, ref, send, recv, k, False, False).start())

    def gather_wait(ref, send, recv):
        each(lambda k: owned(k, lambda: piece(ref, ref, send, recv, k, True, False).wait_recv()))

    def gather_sent(ref, send, recv):
        owner(lambda: each(lambda k: piece(ref, ref, send, recv, k, False, False).wait_send()))

    scatter_start(part.at[0], got1, s1, r1)

    w_copy.wait()
    rows_w = chans * mx * 2
    for b in range(w_v.shape[0] // rows_w):
        wown[b] = w_v[rows_w * b : rows_w * (b + 1), q - q8, :].T

    step = 16
    per = zlines // step

    def local(k, carry):
        y, z = k // per, k % per
        zs = pl.ds(pl.multiple_of(z * step, step), step)
        fields = [f_v[i, y, zs, :] for i in range(chans)]
        for o in range(chans):
            total = fields[0] * pw[0, o] + bias[o]
            for i in range(1, chans):
                total += fields[i] * pw[i, o]
            loc_v[o, y, zs, :] = total
        return carry

    lax.fori_loop(0, ylines * per, local, 0)

    lane = lane_ids(ROWS)
    low_half = lane < LANES // 2
    group = lane % mx

    def take(value, index):
        return jnp.take_along_axis(value, index, axis=1)

    def weights():
        return [wown[b, pl.ds(r0, ROWS), :] for b in range(2 * chans // 2)]

    def mix_first():
        u = scatter_sum(part.at[0], got1, s1, r1)
        ug[pl.ds(me, 1)] = u[None]
        w = weights()
        real = imag = 0.0
        for pair in range(2):
            index = (2 * pair + lane // (LANES // 2)) * mx + group
            ur, ui = take(u, index), take(u, index + LANES // 2)
            wr, wi = w[pair], w[2 + pair]
            real += wr * ur - wi * ui
            imag += wr * ui + wi * ur
        real += pltpu.roll(real, LANES // 2, 1)
        imag += pltpu.roll(imag, LANES // 2, 1)
        mg[pl.ds(me, 1)] = jnp.where(low_half, real, imag)[None]
        gather_start(mg, sm, rm)
        gather_start(ug, su, ru)

    owner(mix_first)
    sy_copy.wait()
    for copy in l_copies:
        copy.wait()
    gather_wait(mg, sm, rm)

    def load_turn(ref):
        m = ref[...].reshape(modes, LANES)
        im = times_i(m)
        turn[0] = m * start_cos[...] + im * start_sin[...]
        turn[1] = im * start_cos[...] - m * start_sin[...]

    load_turn(mg)
    acc[...] = jnp.zeros_like(acc)

    def second(j, carry):
        mode_rhs(turn, rhs)
        synthesise(sy_v, rhs, l_v, spec)
        turn_on(turn, step_cos, step_sin)
        tile_copy(g_hbm, g_v, g_sem, j).wait()

        def cells(k, carry):
            y, z = j * ty + k // per, k % per
            zs = pl.ds(pl.multiple_of(z * step, step), step)
            rows = pl.ds(pl.multiple_of(k * step, step), step)
            for o in range(chans):
                pre = spec[rows, o * nx : (o + 1) * nx] + loc_v[o, y, zs, :]
                up = g_v[o, y, zs, :] * gelu_slope(pre)
                g_v[o, y, zs, :] = up
                high, low = split(up)
                xs[rows, o * nx : (o + 1) * nx] = high
                xs[rows, (chans + o) * nx : (chans + o + 1) * nx] = low
            return carry

        lax.fori_loop(0, ty * per, cells, 0)
        analyse(xs, wt_v, an_v, acc, step_cos, step_sin)
        return carry

    lax.fori_loop(0, steps, second, 0)
    part[1] = spectrum(acc, end_cos, end_sin).reshape(owners, ROWS, LANES)
    scatter_start(part.at[1], got2, s2, r2)

    def out_copy(j):
        rows = pl.ds(j * ty, ty)
        return pltpu.make_async_copy(loc_v.at[:, rows], loc_hbm.at[0, :, rows], out_sem.at[j])

    def back(j, carry):
        def cells(k, carry):
            y, z = j * ty + k // per, k % per
            zs = pl.ds(pl.multiple_of(z * step, step), step)
            ups = [g_v[o, y, zs, :] for o in range(chans)]
            for i in range(chans):
                total = ups[0] * pw[i, 0]
                for o in range(1, chans):
                    total += ups[o] * pw[i, o]
                loc_v[i, y, zs, :] = total
            return carry

        lax.fori_loop(0, ty * per, cells, 0)
        out_copy(j).start()
        return carry

    lax.fori_loop(0, steps, back, 0)

    def mix_second():
        h = scatter_sum(part.at[1], got2, s2, r2)
        hg[pl.ds(me, 1)] = h[None]
        w = weights()
        other = pltpu.roll(h, LANES // 2, 1)
        hr, hi = jnp.where(low_half, h, other), jnp.where(low_half, other, h)
        result = jnp.zeros_like(h)
        for pair in range(2):
            wr, wi = w[pair], w[2 + pair]
            for k, value in enumerate((wr * hr + wi * hi, wr * hi - wi * hr)):
                total = value
                for o in range(1, chans):
                    total += pltpu.roll(value, o * mx, 1)
                chan = lane // mx % chans
                index = chan % 2 * (LANES // 2) + (chans - 1) * mx + group
                here = (lane // (LANES // 2) == k) & (chan // 2 == pair)
                result = jnp.where(here, take(total, index), result)
        ag[pl.ds(me, 1)] = result[None]
        gather_start(ag, sa, ra)
        gather_start(hg, sh, rh)

    owner(mix_second)
    gather_wait(ug, su, ru)
    u_ref[...] = ug[...].reshape(modes, LANES)
    scatter_sent(part.at[0], got1, s1, r1)
    gather_sent(mg, sm, rm)
    gather_sent(ug, su, ru)
    scatter_sent(part.at[1], got2, s2, r2)
    gather_wait(ag, sa, ra)
    a_ref[...] = ag[...].reshape(modes, LANES)
    gather_wait(hg, sh, rh)
    h_ref[...] = hg[...].reshape(modes, LANES)
    gather_sent(ag, sa, ra)
    gather_sent(hg, sh, rh)
    for j in range(steps):
        out_copy(j).wait()


def gradient_kernel(dims, cells_all, a_ref, u_ref, h_ref, ph_ref, loc_ref, l_hbm, sy_ref,
                    o_ref, gs_ref, l_v, spec, turn, rhs, phase, ut, ht, sems):
    chans, mx, my, mz, ylines, zlines, nx, ty, count, cols, owners = dims
    modes = my * mz
    steps = ylines // ty
    j = pl.program_id(0)
    me = lax.axis_index("row") * cols + lax.axis_index("col")

    @pl.when(j == 0)
    def _():
        copies = fill_synthesis(l_hbm, l_v, sems, 0)
        for copy in copies:
            copy.start()
        place = lax.broadcasted_iota(jnp.int32, (modes, count), 1) == me
        found = []
        for k in range(2):
            column = jnp.sum(jnp.where(place, ph_ref[:, k * count : (k + 1) * count], 0.0), axis=1, keepdims=True)
            found.append(jnp.broadcast_to(column, (modes, LANES)))
            phase[k] = jnp.broadcast_to(ph_ref[:, 4 * count + k : 4 * count + k + 1], (modes, LANES))
        m = a_ref[...]
        im = times_i(m)
        turn[0] = m * found[0] + im * found[1]
        turn[1] = im * found[0] - m * found[1]
        ut[...] = u_ref[...].T
        ht[...] = h_ref[...].T
        for copy in copies:
            copy.wait()

    mode_rhs(turn, rhs)
    synthesise(sy_ref, rhs, l_v, spec)
    turn_on(turn, phase.at[0], phase.at[1])
    step = 16
    per = zlines // step

    def cells(k, carry):
        y, z = k // per, k % per
        zs = pl.ds(pl.multiple_of(z * step, step), step)
        rows = pl.ds(pl.multiple_of(k * step, step), step)
        for i in range(chans):
            o_ref[0, i, y, zs, :] = spec[rows, i * nx : (i + 1) * nx] + loc_ref[0, i, y, zs, :]
        return carry

    lax.fori_loop(0, ty * per, cells, 0)

    blocks = 2 * chans * chans // steps
    wave = lax.broadcasted_iota(jnp.int32, (mx, modes), 0)
    factor = jnp.where(wave == 0, 1.0 / cells_all, 2.0 / cells_all).astype(f32)

    def weight(b, carry):
        at = j * blocks + b
        k, i, o = at // (chans * chans), at // chans % chans, at % chans

        def rows_of(ref, kind, c):
            return ref[pl.ds(pl.multiple_of((kind * chans + c) * mx, mx), mx), :]

        ur, ui, hr, hi = rows_of(ut, 0, i), rows_of(ut, 1, i), rows_of(ht, 0, o), rows_of(ht, 1, o)
        value = jnp.where(k == 0, ur * hr + ui * hi, ur * hi - ui * hr) * factor
        out = pl.ds(pl.multiple_of(b * mx, mx), mx)
        for q in range(my):
            lo = q * mz // LANES * LANES
            shift = q * mz - lo
            half = value[:, lo : lo + LANES]
            moved = pltpu.roll(half, LANES - shift, 1) if shift else half
            gs_ref[out, q, :] = moved[:, :mz]
        return carry

    lax.fori_loop(0, blocks, weight, 0)


def solution(mesh):
    nrow, ncol = mesh.shape["row"], mesh.shape["col"]
    count = nrow * ncol

    def per_device(fields, cotangent, spec_weights, point_weights, bias):
        _, chans, ylines, zlines, nx = fields.shape
        _, _, _, mx, my, mz = spec_weights.shape
        ny, nz = ylines * nrow, zlines * ncol
        modes = my * mz
        owners = min(count, modes // ROWS)
        cells_all = float(nx * ny * nz)
        ty = max(1, min(ylines, TILE // zlines))
        steps = ylines // ty
        tile = ty * zlines
        dims = (chans, mx, my, mz, ylines, zlines, nx, ty, count, ncol, owners)
        wt_tab, l_tab = x_tables(chans, nx, mx, cells_all)
        an_tab, sy_tab, ph_tab = yz_tables(ny, nz, my, mz, ty, ylines, zlines, nrow, ncol)
        flat = (2 * chans * chans * mx, my, mz)
        weights = spec_weights.reshape(flat)

        anyspace = pl.BlockSpec(memory_space=pl.ANY)
        vmem = pl.BlockSpec(memory_space=pltpu.VMEM)
        smem = pl.BlockSpec(memory_space=pltpu.SMEM)
        field_shape = jax.ShapeDtypeStruct(fields.shape, f32)
        mode_shape = jax.ShapeDtypeStruct((modes, LANES), f32)
        block = fields.shape[1:]
        gathered = pltpu.VMEM((owners, ROWS, LANES), f32)
        arrived = pltpu.VMEM((count, ROWS, LANES), f32)
        tables = [
            pltpu.VMEM((2 * chans * nx, 2 * LANES), bf16),
            pltpu.VMEM((4 * LANES, chans * nx), bf16),
            pltpu.VMEM((2 * modes, 2 * tile), bf16),
            pltpu.VMEM((tile, 4 * modes), bf16),
        ]
        spec_v = pltpu.VMEM((tile, chans * nx), f32)
        turn_v = pltpu.VMEM((2, modes, LANES), f32)
        rhs_v = pltpu.VMEM((2 * modes, 2 * LANES), bf16)
        dma = pltpu.SemaphoreType.DMA

        local, adjoint, spectrum_u, spectrum_h = pl.pallas_call(
            functools.partial(layer_kernel, dims),
            out_shape=(field_shape, mode_shape, mode_shape, mode_shape),
            in_specs=[anyspace, anyspace, anyspace, smem, smem, anyspace, anyspace, anyspace, anyspace, vmem],
            out_specs=(anyspace, vmem, vmem, vmem),
            scratch_shapes=[
                pltpu.VMEM(block, f32), pltpu.VMEM(block, f32), pltpu.VMEM(block, f32),
                pltpu.VMEM((flat[0], 8, mz), f32),
                pltpu.VMEM((flat[0] // LANES, mz, LANES), f32),
                *tables,
                pltpu.VMEM((tile, 2 * chans * nx), bf16), spec_v,
                pltpu.VMEM((2, modes, LANES), f32), turn_v, rhs_v,
                pltpu.VMEM((6, modes, LANES), f32),
                pltpu.VMEM((2, owners, ROWS, LANES), f32),
                arrived, arrived, gathered, gathered, gathered, gathered,
                dma((steps,)), dma((steps,)), dma((steps,)), dma((9,)),
                *[dma((count,))] * 12,
            ],
            compiler_params=pltpu.CompilerParams(
                collective_id=0, has_side_effects=True, vmem_limit_bytes=60 * 1024 * 1024),
            name="layer",
        )(fields, cotangent, weights, point_weights, bias, wt_tab, l_tab, an_tab, sy_tab, ph_tab)

        def keep(shape):
            return pl.BlockSpec(shape, lambda j: (0,) * len(shape))

        cells = pl.BlockSpec((1, chans, ty, zlines, nx), lambda j: (0, 0, j, 0, 0))
        mode = keep((modes, LANES))
        grad_fields, grad_spectral = pl.pallas_call(
            functools.partial(gradient_kernel, dims, cells_all),
            grid=(steps,),
            out_shape=(field_shape, jax.ShapeDtypeStruct(flat, f32)),
            in_specs=[mode, mode, mode, keep(ph_tab.shape), cells, anyspace, keep(sy_tab.shape)],
            out_specs=(cells, pl.BlockSpec((flat[0] // steps, my, mz), lambda j: (j, 0, 0))),
            scratch_shapes=[
                tables[1], spec_v, turn_v, rhs_v, pltpu.VMEM((2, modes, LANES), f32),
                pltpu.VMEM((LANES, modes), f32), pltpu.VMEM((LANES, modes), f32), dma((4,)),
            ],
            compiler_params=pltpu.CompilerParams(
                dimension_semantics=("arbitrary",), vmem_limit_bytes=56 * 1024 * 1024),
            name="gradients",
        )(adjoint, spectrum_u, spectrum_h, ph_tab, local, l_tab, sy_tab)
        return grad_fields, grad_spectral.reshape(spec_weights.shape)

    placed = (P(None, None, "row", "col", None), P(None, None, "row", "col", None), P(), P(), P())
    return jax.shard_map(
        per_device,
        mesh=mesh,
        in_specs=placed,
        out_specs=(P(None, None, "row", "col", None), P()),
        check_vma=False,
    )
```

time: 108 us -> 86.1 us (0.80)
  Pallas kernels: 99.1 us -> 85.3 us
  local copies, waits for them, and re-layouts: 7.89 us -> 0 us
    pallas_call x5 -> x2, Pallas kernels: 99.1 us -> 85.3 us  [the longest x1 67.1 us: per_device(): pl.pallas_call(functools.partial(layer_kernel, dims), out_shape=(field_sh...]
    reshape x2 -> x0, local copies, waits for them, and re-layouts: 7.89 us -> none  [the longest x1 4.21 us: per_device(): weights = spec_weights.reshape(2, chans, chans, mx, lanes)]
where the time goes in v1:
time: 86.1 us; the launch traced here: 85.9 us
  Pallas kernels  85.3 us (99%)
    pallas_call x1, Pallas kernels, per_device(): pl.pallas_call(functools.partial(layer_kernel, dims), out_shape=(field_sh...  67.1 us
    pallas_call x1, Pallas kernels, per_device(): pl.pallas_call(functools.partial(gradient_kernel, dims, cells_all), grid=...  18.2 us

profile of v1, /device:TPU:0, one launch (start us, length us, event | category | flops | bytes accessed | tf_op | source)
XLA Modules:
  0.0 85.9 jit_solution(12906702021892467534)
XLA Ops:
  0.6 67.1 %layer.1 = (f32[1,4,32,64,256]{4,3,2,1,0:T(8,128)}, f32[256,128]{1,0:T(8,128)}, f32[256,128]{1,0:T(8,128)}, f32[256,128]{1,0:T(8,128)}) custom-call(f32[1,4,32,64,256]{4,3,2,1,0:T(8,128)} %f_hbm.1, f32[1,4,32,64,256]{4,3,2,1,0:T(8,128)} %g_hbm.1, f32[512,16,16]{2,1,0:T(8,128)} %bitcast.2, f32[4,4]{1,0:T(4,128)} %pw.1, f32[4]{0:T(128)} %bias.1, ...), custom_call_target="tpu_custom_call" | custom-call | tf_op jit(solution)/shard_map/layer/pallas_call | solution.py:525
  67.8 18.2 %gradients.1 = (f32[1,4,32,64,256]{4,3,2,1,0:T(8,128)}, f32[512,16,16]{2,1,0:T(8,128)}) custom-call(f32[256,128]{1,0:T(8,128)} %get-tuple-element.8.a_ref, f32[256,128]{1,0:T(8,128)} %get-tuple-element.9.u_ref, f32[256,128]{1,0:T(8,128)} %get-tuple-element.10.h_ref, f32[256,130]{1,0:T(8,128)} %constant.14.clone.ph_ref, ...), custom_call_target="tpu_custom_call" | custom-call | tf_op jit(solution)/shard_map/gradients/pallas_call | solution.py:553

commit v2 on v1

--- a/solution.py
+++ b/solution.py
@@ -37,11 +37,13 @@
 def x_tables(chans, length, modes, cells):
     angle = 2.0 * np.pi / length * ((np.arange(length)[:, None] * np.arange(modes)) % length)
     weight = np.where(np.arange(modes) == 0, 1.0, 2.0) / cells
-    eye = np.eye(chans)
     first = np.stack([np.cos(angle), -np.sin(angle)], 1)
-    wide = np.einsum("cd,xkp->cxkdp", eye, first).reshape(chans * length, -1)
-    tall = np.einsum("cd,xkp->kcpdx", eye, first * weight).reshape(-1, chans * length)
-    return np.concatenate(split_np(wide), 1), np.concatenate(split_np(tall), 0)
+    eye = np.eye(chans).reshape(chans, chans // 2, 2)
+    wide = np.einsum("cgd,xkp->cxgkdp", eye, first).reshape(chans, 1, length, -1)
+    wide = np.repeat(wide, 2, 1).reshape(2 * chans * length, -1)
+    tall = np.einsum("de,xkp->kdpex", np.eye(2), first * weight).reshape(-1, 2 * length)
+    high, low = split_np(tall)
+    return np.concatenate(split_np(wide), 1), np.concatenate([high, high, low, 0 * low], 0)
 
 
 def yz_tables(ny, nz, my, mz, ty, ylines, zlines, nrow, ncol):
@@ -72,12 +74,21 @@
 
 
 def times_i(value):
-    turned = pltpu.roll(value, LANES // 2, 1)
-    return jnp.where(lane_ids(value.shape[0]) < LANES // 2, -turned, turned)
-
-
-def analyse(xs, wt_v, an_v, acc, step_cos, step_sin):
-    pairs = dot(xs[...], wt_v[...])
+    quarter = LANES // 4
+    real = lane_ids(value.shape[0]) % (LANES // 2) < quarter
+    return jnp.where(real, -pltpu.roll(value, LANES - quarter, 1), pltpu.roll(value, quarter, 1))
+
+
+def along_x(value, c, xs, wt_v):
+    width = value.shape[1]
+    at = 2 * c * width
+    high, low = split(value)
+    xs[:, at : at + width] = high
+    xs[:, at + width : at + 2 * width] = low
+    return dot(xs[:, at : at + 2 * width], wt_v[at : at + 2 * width, :])
+
+
+def analyse(pairs, an_v, acc, step_cos, step_sin):
     part = jnp.concatenate(split(pairs[:, :LANES] + pairs[:, LANES:]), 1)
     both = dot(an_v[...], jnp.concatenate([part, part], 0))
     both = both[:, :LANES] + both[:, LANES:]
@@ -110,10 +121,22 @@
     turn[1] = im * step_cos[...] - m * step_sin[...]
 
 
-def synthesise(sy_v, rhs, l_v, spec):
+def synthesise(sy_v, rhs, lhs):
     pairs = dot(sy_v[...], jnp.concatenate([rhs[...], rhs[...]], 0))
-    high, low = split(pairs[:, :LANES] + pairs[:, LANES:])
-    spec[...] = dot(jnp.concatenate([high, low, high, low], 1), l_v[...])
+    value = pairs[:, :LANES] + pairs[:, LANES:]
+    other = pltpu.roll(value, LANES // 2, 1)
+    lower = lane_ids(value.shape[0]) < LANES // 2
+    for pair in range(2):
+        twice = jnp.where(lower, value, other) if pair == 0 else jnp.where(lower, other, value)
+        high = twice.astype(bf16)
+        wide = high.astype(f32)
+        lhs[pair, :, :LANES] = jnp.where(lower, wide, twice - wide).astype(bf16)
+        lhs[pair, :, LANES:] = high
+
+
+def back_to_x(lhs, l_v, c):
+    nx = l_v.shape[1] // 2
+    return dot(lhs[c // 2], l_v[:, c % 2 * nx : (c % 2 + 1) * nx])
 
 
 def gelu_slope(v):
@@ -122,30 +145,16 @@
     return (0.5 * lax.erf(arg) + 0.5) + (v * (1.0 / math.sqrt(2.0 * math.pi))) * gauss
 
 
-def fill_twice(src, dst, sems, at):
-    rows, out = src.shape[0], []
-    for k in range(2):
-        out.append(pltpu.make_async_copy(src, dst.at[pl.ds(k * rows, rows)], sems.at[at + k]))
-    return out
-
-
-def fill_synthesis(src, dst, sems, at):
-    rows, out = src.shape[0] // 2, []
-    for k in range(4):
-        out.append(pltpu.make_async_copy(
-            src.at[pl.ds(k // 2 * rows, rows)], dst.at[pl.ds(k * rows, rows)], sems.at[at + k]))
-    return out
-
-
 def layer_kernel(dims, f_hbm, g_hbm, w_hbm, pw, bias, wt_hbm, l_hbm, an_hbm, sy_hbm, ph_ref,
                  loc_hbm, a_ref, u_ref, h_ref,
-                 f_v, g_v, loc_v, w_v, wown, wt_v, l_v, an_v, sy_v, xs, spec, acc, turn, rhs,
+                 f_v, g_v, loc_v, w_v, wown, wt_v, l_v, an_v, sy_v, xs, lhs, acc, turn, rhs,
                  phase, part, got1, got2, mg, ug, ag, hg,
                  f_sem, g_sem, out_sem, tab_sem,
                  s1, r1, sm, rm, su, ru, s2, r2, sa, ra, sh, rh):
     chans, mx, my, mz, ylines, zlines, nx, ty, count, cols, owners = dims
     modes = my * mz
     steps = ylines // ty
+    tile = ty * zlines
     me = lax.axis_index("row") * cols + lax.axis_index("col")
 
     def device(t):
@@ -167,21 +176,19 @@
         rows = pl.ds(j * ty, ty)
         return pltpu.make_async_copy(src.at[0, :, rows], dst.at[:, rows], sem.at[j])
 
-    wt_copies = fill_twice(wt_hbm, wt_v, tab_sem, 0)
-    l_copies = fill_synthesis(l_hbm, l_v, tab_sem, 2)
-    an_copy = pltpu.make_async_copy(an_hbm, an_v, tab_sem.at[6])
-    sy_copy = pltpu.make_async_copy(sy_hbm, sy_v, tab_sem.at[7])
-    w_copy = pltpu.make_async_copy(w_hbm.at[:, pl.ds(q8, 8), :], w_v, tab_sem.at[8])
-    for copy in wt_copies:
-        copy.start()
+    wt_copy = pltpu.make_async_copy(wt_hbm, wt_v, tab_sem.at[0])
+    l_copy = pltpu.make_async_copy(l_hbm, l_v, tab_sem.at[1])
+    an_copy = pltpu.make_async_copy(an_hbm, an_v, tab_sem.at[2])
+    sy_copy = pltpu.make_async_copy(sy_hbm, sy_v, tab_sem.at[3])
+    w_copy = pltpu.make_async_copy(w_hbm.at[:, pl.ds(q8, 8), :], w_v, tab_sem.at[4])
+    wt_copy.start()
     tile_copy(f_hbm, f_v, f_sem, 0).start()
     an_copy.start()
     for j in range(1, steps):
         tile_copy(f_hbm, f_v, f_sem, j).start()
     w_copy.start()
     sy_copy.start()
-    for copy in l_copies:
-        copy.start()
+    l_copy.start()
     for j in range(steps):
         tile_copy(g_hbm, g_v, g_sem, j).start()
 
@@ -194,23 +201,16 @@
     start_cos, start_sin, end_cos, end_sin, step_cos, step_sin = [phase.at[k] for k in range(6)]
     acc[...] = jnp.zeros_like(acc)
 
-    for copy in wt_copies:
-        copy.wait()
+    wt_copy.wait()
     an_copy.wait()
 
     def first(j, carry):
         tile_copy(f_hbm, f_v, f_sem, j).wait()
 
-        def cut(k, carry):
-            rows = pl.ds(pl.multiple_of(k * zlines, zlines), zlines)
-            for c in range(chans):
-                high, low = split(f_v[c, j * ty + k])
-                xs[rows, c * nx : (c + 1) * nx] = high
-                xs[rows, (chans + c) * nx : (chans + c + 1) * nx] = low
-            return carry
-
-        lax.fori_loop(0, ty, cut, 0)
-        analyse(xs, wt_v, an_v, acc, step_cos, step_sin)
+        pairs = 0.0
+        for c in range(chans):
+            pairs += along_x(f_v[c, pl.ds(j * ty, ty)].reshape(tile, nx), c, xs, wt_v)
+        analyse(pairs, an_v, acc, step_cos, step_sin)
         return carry
 
     lax.fori_loop(0, steps, first, 0)
@@ -286,8 +286,12 @@
     lax.fori_loop(0, ylines * per, local, 0)
 
     lane = lane_ids(ROWS)
-    low_half = lane < LANES // 2
-    group = lane % mx
+    quarter = LANES // 4
+    is_real = lane % (LANES // 2) < quarter
+    wave = lane % mx
+
+    def lane_of(kind, chan):
+        return chan // 2 * (LANES // 2) + kind * quarter + chan % 2 * mx + wave
 
     def take(value, index):
         return jnp.take_along_axis(value, index, axis=1)
@@ -301,21 +305,21 @@
         w = weights()
         real = imag = 0.0
         for pair in range(2):
-            index = (2 * pair + lane // (LANES // 2)) * mx + group
-            ur, ui = take(u, index), take(u, index + LANES // 2)
+            chan = 2 * pair + lane // (LANES // 2)
+            ur, ui = take(u, lane_of(0, chan)), take(u, lane_of(1, chan))
             wr, wi = w[pair], w[2 + pair]
             real += wr * ur - wi * ui
             imag += wr * ui + wi * ur
         real += pltpu.roll(real, LANES // 2, 1)
         imag += pltpu.roll(imag, LANES // 2, 1)
-        mg[pl.ds(me, 1)] = jnp.where(low_half, real, imag)[None]
+        source = lane // (LANES // 2) * quarter + lane % quarter
+        mg[pl.ds(me, 1)] = jnp.where(is_real, take(real, source), take(imag, source))[None]
         gather_start(mg, sm, rm)
         gather_start(ug, su, ru)
 
     owner(mix_first)
     sy_copy.wait()
-    for copy in l_copies:
-        copy.wait()
+    l_copy.wait()
     gather_wait(mg, sm, rm)
 
     def load_turn(ref):
@@ -329,25 +333,17 @@
 
     def second(j, carry):
         mode_rhs(turn, rhs)
-        synthesise(sy_v, rhs, l_v, spec)
+        synthesise(sy_v, rhs, lhs)
         turn_on(turn, step_cos, step_sin)
         tile_copy(g_hbm, g_v, g_sem, j).wait()
-
-        def cells(k, carry):
-            y, z = j * ty + k // per, k % per
-            zs = pl.ds(pl.multiple_of(z * step, step), step)
-            rows = pl.ds(pl.multiple_of(k * step, step), step)
-            for o in range(chans):
-                pre = spec[rows, o * nx : (o + 1) * nx] + loc_v[o, y, zs, :]
-                up = g_v[o, y, zs, :] * gelu_slope(pre)
-                g_v[o, y, zs, :] = up
-                high, low = split(up)
-                xs[rows, o * nx : (o + 1) * nx] = high
-                xs[rows, (chans + o) * nx : (chans + o + 1) * nx] = low
-            return carry
-
-        lax.fori_loop(0, ty * per, cells, 0)
-        analyse(xs, wt_v, an_v, acc, step_cos, step_sin)
+        lines = pl.ds(j * ty, ty)
+        pairs = 0.0
+        for o in range(chans):
+            pre = back_to_x(lhs, l_v, o) + loc_v[o, lines].reshape(tile, nx)
+            up = g_v[o, lines].reshape(tile, nx) * gelu_slope(pre)
+            g_v[o, lines] = up.reshape(ty, zlines, nx)
+            pairs += along_x(up, o, xs, wt_v)
+        analyse(pairs, an_v, acc, step_cos, step_sin)
         return carry
 
     lax.fori_loop(0, steps, second, 0)
@@ -380,8 +376,8 @@
         h = scatter_sum(part.at[1], got2, s2, r2)
         hg[pl.ds(me, 1)] = h[None]
         w = weights()
-        other = pltpu.roll(h, LANES // 2, 1)
-        hr, hi = jnp.where(low_half, h, other), jnp.where(low_half, other, h)
+        chan = lane // mx % chans
+        hr, hi = take(h, lane_of(0, chan)), take(h, lane_of(1, chan))
         result = jnp.zeros_like(h)
         for pair in range(2):
             wr, wi = w[pair], w[2 + pair]
@@ -389,9 +385,8 @@
                 total = value
                 for o in range(1, chans):
                     total += pltpu.roll(value, o * mx, 1)
-                chan = lane // mx % chans
-                index = chan % 2 * (LANES // 2) + (chans - 1) * mx + group
-                here = (lane // (LANES // 2) == k) & (chan // 2 == pair)
+                index = lane % quarter // mx * (LANES // 2) + (chans - 1) * mx + wave
+                here = (is_real if k == 0 else jnp.logical_not(is_real)) & (lane // (LANES // 2) == pair)
                 result = jnp.where(here, take(total, index), result)
         ag[pl.ds(me, 1)] = result[None]
         gather_start(ag, sa, ra)
@@ -414,8 +409,8 @@
         out_copy(j).wait()
 
 
-def gradient_kernel(dims, cells_all, a_ref, u_ref, h_ref, ph_ref, loc_ref, l_hbm, sy_ref,
-                    o_ref, gs_ref, l_v, spec, turn, rhs, phase, ut, ht, sems):
+def gradient_kernel(dims, cells_all, a_ref, u_ref, h_ref, ph_ref, loc_ref, l_ref, sy_ref,
+                    o_ref, gs_ref, lhs, turn, rhs, phase, ut, ht):
     chans, mx, my, mz, ylines, zlines, nx, ty, count, cols, owners = dims
     modes = my * mz
     steps = ylines // ty
@@ -424,9 +419,6 @@
 
     @pl.when(j == 0)
     def _():
-        copies = fill_synthesis(l_hbm, l_v, sems, 0)
-        for copy in copies:
-            copy.start()
         place = lax.broadcasted_iota(jnp.int32, (modes, count), 1) == me
         found = []
         for k in range(2):
@@ -439,48 +431,37 @@
         turn[1] = im * found[0] - m * found[1]
         ut[...] = u_ref[...].T
         ht[...] = h_ref[...].T
-        for copy in copies:
-            copy.wait()
 
     mode_rhs(turn, rhs)
-    synthesise(sy_ref, rhs, l_v, spec)
+    synthesise(sy_ref, rhs, lhs)
     turn_on(turn, phase.at[0], phase.at[1])
-    step = 16
-    per = zlines // step
-
-    def cells(k, carry):
-        y, z = k // per, k % per
-        zs = pl.ds(pl.multiple_of(z * step, step), step)
-        rows = pl.ds(pl.multiple_of(k * step, step), step)
-        for i in range(chans):
-            o_ref[0, i, y, zs, :] = spec[rows, i * nx : (i + 1) * nx] + loc_ref[0, i, y, zs, :]
-        return carry
-
-    lax.fori_loop(0, ty * per, cells, 0)
-
     blocks = 2 * chans * chans // steps
     wave = lax.broadcasted_iota(jnp.int32, (mx, modes), 0)
     factor = jnp.where(wave == 0, 1.0 / cells_all, 2.0 / cells_all).astype(f32)
 
-    def weight(b, carry):
+    def weight(b):
         at = j * blocks + b
         k, i, o = at // (chans * chans), at // chans % chans, at % chans
 
         def rows_of(ref, kind, c):
-            return ref[pl.ds(pl.multiple_of((kind * chans + c) * mx, mx), mx), :]
+            row = (c // 2 * 4 + kind * 2 + c % 2) * mx
+            return ref[pl.ds(pl.multiple_of(row, mx), mx), :]
 
         ur, ui, hr, hi = rows_of(ut, 0, i), rows_of(ut, 1, i), rows_of(ht, 0, o), rows_of(ht, 1, o)
         value = jnp.where(k == 0, ur * hr + ui * hi, ur * hi - ui * hr) * factor
-        out = pl.ds(pl.multiple_of(b * mx, mx), mx)
         for q in range(my):
             lo = q * mz // LANES * LANES
             shift = q * mz - lo
             half = value[:, lo : lo + LANES]
             moved = pltpu.roll(half, LANES - shift, 1) if shift else half
-            gs_ref[out, q, :] = moved[:, :mz]
-        return carry
-
-    lax.fori_loop(0, blocks, weight, 0)
+            gs_ref[b * mx : (b + 1) * mx, q, :] = moved[:, :mz]
+
+    share = -(-blocks // chans)
+    for i in range(chans):
+        out = back_to_x(lhs, l_ref, i)
+        o_ref[0, i] = loc_ref[0, i] + out.reshape(ty, zlines, nx)
+        for b in range(i * share, min((i + 1) * share, blocks)):
+            weight(b)
 
 
 def solution(mesh):
@@ -513,11 +494,11 @@
         arrived = pltpu.VMEM((count, ROWS, LANES), f32)
         tables = [
             pltpu.VMEM((2 * chans * nx, 2 * LANES), bf16),
-            pltpu.VMEM((4 * LANES, chans * nx), bf16),
+            pltpu.VMEM((2 * LANES, 2 * nx), bf16),
             pltpu.VMEM((2 * modes, 2 * tile), bf16),
             pltpu.VMEM((tile, 4 * modes), bf16),
         ]
-        spec_v = pltpu.VMEM((tile, chans * nx), f32)
+        lhs_v = pltpu.VMEM((2, tile, 2 * LANES), bf16)
         turn_v = pltpu.VMEM((2, modes, LANES), f32)
         rhs_v = pltpu.VMEM((2 * modes, 2 * LANES), bf16)
         dma = pltpu.SemaphoreType.DMA
@@ -532,12 +513,12 @@
                 pltpu.VMEM((flat[0], 8, mz), f32),
                 pltpu.VMEM((flat[0] // LANES, mz, LANES), f32),
                 *tables,
-                pltpu.VMEM((tile, 2 * chans * nx), bf16), spec_v,
+                pltpu.VMEM((tile, 2 * chans * nx), bf16), lhs_v,
                 pltpu.VMEM((2, modes, LANES), f32), turn_v, rhs_v,
                 pltpu.VMEM((6, modes, LANES), f32),
                 pltpu.VMEM((2, owners, ROWS, LANES), f32),
                 arrived, arrived, gathered, gathered, gathered, gathered,
-                dma((steps,)), dma((steps,)), dma((steps,)), dma((9,)),
+                dma((steps,)), dma((steps,)), dma((steps,)), dma((5,)),
                 *[dma((count,))] * 12,
             ],
             compiler_params=pltpu.CompilerParams(
@@ -554,11 +535,11 @@
             functools.partial(gradient_kernel, dims, cells_all),
             grid=(steps,),
             out_shape=(field_shape, jax.ShapeDtypeStruct(flat, f32)),
-            in_specs=[mode, mode, mode, keep(ph_tab.shape), cells, anyspace, keep(sy_tab.shape)],
+            in_specs=[mode, mode, mode, keep(ph_tab.shape), cells, keep(l_tab.shape), keep(sy_tab.shape)],
             out_specs=(cells, pl.BlockSpec((flat[0] // steps, my, mz), lambda j: (j, 0, 0))),
             scratch_shapes=[
-                tables[1], spec_v, turn_v, rhs_v, pltpu.VMEM((2, modes, LANES), f32),
-                pltpu.VMEM((LANES, modes), f32), pltpu.VMEM((LANES, modes), f32), dma((4,)),
+                lhs_v, turn_v, rhs_v, pltpu.VMEM((2, modes, LANES), f32),
+                pltpu.VMEM((LANES, modes), f32), pltpu.VMEM((LANES, modes), f32),
             ],
             compiler_params=pltpu.CompilerParams(
                 dimension_semantics=("arbitrary",), vmem_limit_bytes=56 * 1024 * 1024),

time: 86.1 us -> 73.5 us (0.85)
  Pallas kernels: 85.3 us -> 72.6 us
    pallas_call x1, Pallas kernels: 67.1 us -> 60.1 us  [per_device(): pl.pallas_call(functools.partial(layer_kernel, dims), out_shape=(field_sh...]
    pallas_call x1, Pallas kernels: 18.2 us -> 12.5 us  [per_device(): pl.pallas_call(functools.partial(gradient_kernel, dims, cells_all), grid=...]
where the time goes in v2:
time: 73.5 us; the launch traced here: 73.3 us
  Pallas kernels  72.6 us (99%)
    pallas_call x1, Pallas kernels, per_device(): pl.pallas_call(functools.partial(layer_kernel, dims), out_shape=(field_sh...  60.1 us
    pallas_call x1, Pallas kernels, per_device(): pl.pallas_call(functools.partial(gradient_kernel, dims, cells_all), grid=...  12.5 us

profile of v2, /device:TPU:0, one launch (start us, length us, event | category | flops | bytes accessed | tf_op | source)
XLA Modules:
  0.0 73.3 jit_solution(8169017359851305272)
XLA Ops:
  0.6 60.1 %layer.1 = (f32[1,4,32,64,256]{4,3,2,1,0:T(8,128)}, f32[256,128]{1,0:T(8,128)}, f32[256,128]{1,0:T(8,128)}, f32[256,128]{1,0:T(8,128)}) custom-call(f32[1,4,32,64,256]{4,3,2,1,0:T(8,128)} %f_hbm.1, f32[1,4,32,64,256]{4,3,2,1,0:T(8,128)} %g_hbm.1, f32[512,16,16]{2,1,0:T(8,128)} %bitcast.2, f32[4,4]{1,0:T(4,128)} %pw.1, f32[4]{0:T(128)} %bias.1, ...), custom_call_target="tpu_custom_call" | custom-call | tf_op jit(solution)/shard_map/layer/pallas_call | solution.py:506
  60.8 12.5 %gradients.1 = (f32[1,4,32,64,256]{4,3,2,1,0:T(8,128)}, f32[512,16,16]{2,1,0:T(8,128)}) custom-call(f32[256,128]{1,0:T(8,128)} %get-tuple-element.8.a_ref, f32[256,128]{1,0:T(8,128)} %get-tuple-element.9.u_ref, f32[256,128]{1,0:T(8,128)} %get-tuple-element.10.h_ref, f32[256,130]{1,0:T(8,128)} %constant.14.clone.ph_ref, ...), custom_call_target="tpu_custom_call" | custom-call | tf_op jit(solution)/shard_map/gradients/pallas_call | solution.py:534

commit v3 on v2

--- a/solution.py
+++ b/solution.py
@@ -146,15 +146,16 @@
 
 
 def layer_kernel(dims, f_hbm, g_hbm, w_hbm, pw, bias, wt_hbm, l_hbm, an_hbm, sy_hbm, ph_ref,
-                 loc_hbm, a_ref, u_ref, h_ref,
-                 f_v, g_v, loc_v, w_v, wown, wt_v, l_v, an_v, sy_v, xs, lhs, acc, turn, rhs,
-                 phase, part, got1, got2, mg, ug, ag, hg,
-                 f_sem, g_sem, out_sem, tab_sem,
-                 s1, r1, sm, rm, su, ru, s2, r2, sa, ra, sh, rh):
+                 loc_o, u_ref, h_ref, wd_ref,
+                 f_v, g_v, w_v, wt_v, l_v, an_v, sy_v, xs, lhs, acc, turn, rhs,
+                 phase, part, got1, got2, mg, ug, hg,
+                 f_sem, g_sem, tab_sem,
+                 s1, r1, sm, rm, su, ru, s2, r2, sh, rh):
     chans, mx, my, mz, ylines, zlines, nx, ty, count, cols, owners = dims
     modes = my * mz
     steps = ylines // ty
     tile = ty * zlines
+    loc_v = loc_o.at[0]
     me = lax.axis_index("row") * cols + lax.axis_index("col")
 
     def device(t):
@@ -170,7 +171,6 @@
 
     q = jnp.minimum(me, owners - 1) * ROWS // mz
     r0 = pl.multiple_of(lax.rem(jnp.minimum(me, owners - 1) * ROWS, mz), ROWS)
-    q8 = pl.multiple_of(q // 8 * 8, 8)
 
     def tile_copy(src, dst, sem, j):
         rows = pl.ds(j * ty, ty)
@@ -180,7 +180,7 @@
     l_copy = pltpu.make_async_copy(l_hbm, l_v, tab_sem.at[1])
     an_copy = pltpu.make_async_copy(an_hbm, an_v, tab_sem.at[2])
     sy_copy = pltpu.make_async_copy(sy_hbm, sy_v, tab_sem.at[3])
-    w_copy = pltpu.make_async_copy(w_hbm.at[:, pl.ds(q8, 8), :], w_v, tab_sem.at[4])
+    w_copy = pltpu.make_async_copy(w_hbm, w_v, tab_sem.at[4])
     wt_copy.start()
     tile_copy(f_hbm, f_v, f_sem, 0).start()
     an_copy.start()
@@ -267,7 +267,7 @@
     w_copy.wait()
     rows_w = chans * mx * 2
     for b in range(w_v.shape[0] // rows_w):
-        wown[b] = w_v[rows_w * b : rows_w * (b + 1), q - q8, :].T
+        wd_ref[b, pl.ds(pl.multiple_of(q * mz, mz), mz), :] = w_v[rows_w * b : rows_w * (b + 1), q, :].T
 
     step = 16
     per = zlines // step
@@ -297,7 +297,7 @@
         return jnp.take_along_axis(value, index, axis=1)
 
     def weights():
-        return [wown[b, pl.ds(r0, ROWS), :] for b in range(2 * chans // 2)]
+        return [wd_ref[b, pl.ds(pl.multiple_of(q * mz + r0, ROWS), ROWS), :] for b in range(chans)]
 
     def mix_first():
         u = scatter_sum(part.at[0], got1, s1, r1)
@@ -318,6 +318,14 @@
         gather_start(ug, su, ru)
 
     owner(mix_first)
+
+    def relay(k, carry):
+        row = pl.multiple_of(k * mz, mz)
+        for b in range(chans):
+            wd_ref[b, pl.ds(row, mz), :] = w_v[rows_w * b : rows_w * (b + 1), k, :].T
+        return carry
+
+    lax.fori_loop(0, my, relay, 0)
     sy_copy.wait()
     l_copy.wait()
     gather_wait(mg, sm, rm)
@@ -350,10 +358,6 @@
     part[1] = spectrum(acc, end_cos, end_sin).reshape(owners, ROWS, LANES)
     scatter_start(part.at[1], got2, s2, r2)
 
-    def out_copy(j):
-        rows = pl.ds(j * ty, ty)
-        return pltpu.make_async_copy(loc_v.at[:, rows], loc_hbm.at[0, :, rows], out_sem.at[j])
-
     def back(j, carry):
         def cells(k, carry):
             y, z = j * ty + k // per, k % per
@@ -367,49 +371,54 @@
             return carry
 
         lax.fori_loop(0, ty * per, cells, 0)
-        out_copy(j).start()
         return carry
 
     lax.fori_loop(0, steps, back, 0)
 
-    def mix_second():
-        h = scatter_sum(part.at[1], got2, s2, r2)
-        hg[pl.ds(me, 1)] = h[None]
-        w = weights()
-        chan = lane // mx % chans
-        hr, hi = take(h, lane_of(0, chan)), take(h, lane_of(1, chan))
-        result = jnp.zeros_like(h)
-        for pair in range(2):
-            wr, wi = w[pair], w[2 + pair]
-            for k, value in enumerate((wr * hr + wi * hi, wr * hi - wi * hr)):
-                total = value
-                for o in range(1, chans):
-                    total += pltpu.roll(value, o * mx, 1)
-                index = lane % quarter // mx * (LANES // 2) + (chans - 1) * mx + wave
-                here = (is_real if k == 0 else jnp.logical_not(is_real)) & (lane // (LANES // 2) == pair)
-                result = jnp.where(here, take(total, index), result)
-        ag[pl.ds(me, 1)] = result[None]
-        gather_start(ag, sa, ra)
+    def last():
+        hg[pl.ds(me, 1)] = scatter_sum(part.at[1], got2, s2, r2)[None]
         gather_start(hg, sh, rh)
 
-    owner(mix_second)
+    owner(last)
     gather_wait(ug, su, ru)
     u_ref[...] = ug[...].reshape(modes, LANES)
     scatter_sent(part.at[0], got1, s1, r1)
     gather_sent(mg, sm, rm)
     gather_sent(ug, su, ru)
     scatter_sent(part.at[1], got2, s2, r2)
-    gather_wait(ag, sa, ra)
-    a_ref[...] = ag[...].reshape(modes, LANES)
     gather_wait(hg, sh, rh)
     h_ref[...] = hg[...].reshape(modes, LANES)
-    gather_sent(ag, sa, ra)
     gather_sent(hg, sh, rh)
-    for j in range(steps):
-        out_copy(j).wait()
-
-
-def gradient_kernel(dims, cells_all, a_ref, u_ref, h_ref, ph_ref, loc_ref, l_ref, sy_ref,
+
+
+def lane_of(kind, chan, wave, width):
+    return chan // 2 * (LANES // 2) + kind * (LANES // 4) + chan % 2 * width + wave
+
+
+def adjoint(h, weights, chans, mx):
+    lane = lane_ids(h.shape[0])
+    wave, quarter = lane % mx, LANES // 4
+    is_real = lane % (LANES // 2) < quarter
+
+    def take(value, index):
+        return jnp.take_along_axis(value, index, axis=1)
+
+    chan = lane // mx % chans
+    hr, hi = take(h, lane_of(0, chan, wave, mx)), take(h, lane_of(1, chan, wave, mx))
+    index = lane % quarter // mx * (LANES // 2) + (chans - 1) * mx + wave
+    result = jnp.zeros_like(h)
+    for pair in range(2):
+        wr, wi = weights[pair], weights[2 + pair]
+        for k, value in enumerate((wr * hr + wi * hi, wr * hi - wi * hr)):
+            total = value
+            for o in range(1, chans):
+                total += pltpu.roll(value, o * mx, 1)
+            here = (is_real if k == 0 else jnp.logical_not(is_real)) & (lane // (LANES // 2) == pair)
+            result = jnp.where(here, take(total, index), result)
+    return result
+
+
+def gradient_kernel(dims, cells_all, u_ref, h_ref, wd_ref, ph_ref, loc_ref, l_ref, sy_ref,
                     o_ref, gs_ref, lhs, turn, rhs, phase, ut, ht):
     chans, mx, my, mz, ylines, zlines, nx, ty, count, cols, owners = dims
     modes = my * mz
@@ -425,7 +434,7 @@
             column = jnp.sum(jnp.where(place, ph_ref[:, k * count : (k + 1) * count], 0.0), axis=1, keepdims=True)
             found.append(jnp.broadcast_to(column, (modes, LANES)))
             phase[k] = jnp.broadcast_to(ph_ref[:, 4 * count + k : 4 * count + k + 1], (modes, LANES))
-        m = a_ref[...]
+        m = adjoint(h_ref[...], [wd_ref[b] for b in range(chans)], chans, mx)
         im = times_i(m)
         turn[0] = m * found[0] + im * found[1]
         turn[1] = im * found[0] - m * found[1]
@@ -459,7 +468,7 @@
     share = -(-blocks // chans)
     for i in range(chans):
         out = back_to_x(lhs, l_ref, i)
-        o_ref[0, i] = loc_ref[0, i] + out.reshape(ty, zlines, nx)
+        o_ref[0, i] = loc_ref[0, i, pl.ds(j * ty, ty)] + out.reshape(ty, zlines, nx)
         for b in range(i * share, min((i + 1) * share, blocks)):
             weight(b)
 
@@ -503,28 +512,30 @@
         rhs_v = pltpu.VMEM((2 * modes, 2 * LANES), bf16)
         dma = pltpu.SemaphoreType.DMA
 
-        local, adjoint, spectrum_u, spectrum_h = pl.pallas_call(
+        local, spectrum_u, spectrum_h, wide_w = pl.pallas_call(
             functools.partial(layer_kernel, dims),
-            out_shape=(field_shape, mode_shape, mode_shape, mode_shape),
+            out_shape=(pltpu.VMEM(fields.shape, f32),) + (pltpu.VMEM((modes, LANES), f32),) * 2
+            + (pltpu.VMEM((4, modes, LANES), f32),),
             in_specs=[anyspace, anyspace, anyspace, smem, smem, anyspace, anyspace, anyspace, anyspace, vmem],
-            out_specs=(anyspace, vmem, vmem, vmem),
+            out_specs=(vmem, vmem, vmem, vmem),
             scratch_shapes=[
-                pltpu.VMEM(block, f32), pltpu.VMEM(block, f32), pltpu.VMEM(block, f32),
-                pltpu.VMEM((flat[0], 8, mz), f32),
-                pltpu.VMEM((flat[0] // LANES, mz, LANES), f32),
+                pltpu.VMEM(block, f32), pltpu.VMEM(block, f32),
+                pltpu.VMEM(flat, f32),
                 *tables,
                 pltpu.VMEM((tile, 2 * chans * nx), bf16), lhs_v,
                 pltpu.VMEM((2, modes, LANES), f32), turn_v, rhs_v,
                 pltpu.VMEM((6, modes, LANES), f32),
                 pltpu.VMEM((2, owners, ROWS, LANES), f32),
-                arrived, arrived, gathered, gathered, gathered, gathered,
-                dma((steps,)), dma((steps,)), dma((steps,)), dma((5,)),
-                *[dma((count,))] * 12,
+                arrived, arrived, gathered, gathered, gathered,
+                dma((steps,)), dma((steps,)), dma((5,)),
+                *[dma((count,))] * 10,
             ],
             compiler_params=pltpu.CompilerParams(
-                collective_id=0, has_side_effects=True, vmem_limit_bytes=60 * 1024 * 1024),
+                collective_id=0, has_side_effects=True, vmem_limit_bytes=46 * 1024 * 1024),
             name="layer",
-        )(fields, cotangent, weights, point_weights, bias, wt_tab, l_tab, an_tab, sy_tab, ph_tab)
+        )(*[pltpu.with_memory_space_constraint(x, pltpu.HBM) for x in (fields, cotangent, weights)],
+          point_weights, bias,
+          *[pltpu.with_memory_space_constraint(jnp.asarray(x), pltpu.HBM) for x in (wt_tab, l_tab, an_tab, sy_tab)], ph_tab)
 
         def keep(shape):
             return pl.BlockSpec(shape, lambda j: (0,) * len(shape))
@@ -535,16 +546,16 @@
             functools.partial(gradient_kernel, dims, cells_all),
             grid=(steps,),
             out_shape=(field_shape, jax.ShapeDtypeStruct(flat, f32)),
-            in_specs=[mode, mode, mode, keep(ph_tab.shape), cells, keep(l_tab.shape), keep(sy_tab.shape)],
+            in_specs=[mode, mode, keep((4, modes, LANES)), keep(ph_tab.shape), vmem, keep(l_tab.shape), keep(sy_tab.shape)],
             out_specs=(cells, pl.BlockSpec((flat[0] // steps, my, mz), lambda j: (j, 0, 0))),
             scratch_shapes=[
                 lhs_v, turn_v, rhs_v, pltpu.VMEM((2, modes, LANES), f32),
                 pltpu.VMEM((LANES, modes), f32), pltpu.VMEM((LANES, modes), f32),
             ],
             compiler_params=pltpu.CompilerParams(
-                dimension_semantics=("arbitrary",), vmem_limit_bytes=56 * 1024 * 1024),
+                dimension_semantics=("arbitrary",), vmem_limit_bytes=36 * 1024 * 1024),
             name="gradients",
-        )(adjoint, spectrum_u, spectrum_h, ph_tab, local, l_tab, sy_tab)
+        )(spectrum_u, spectrum_h, wide_w, ph_tab, local, l_tab, sy_tab)
         return grad_fields, grad_spectral.reshape(spec_weights.shape)
 
     placed = (P(None, None, "row", "col", None), P(None, None, "row", "col", None), P(), P(), P())

time: 73.5 us -> 64.8 us (0.88)
  Pallas kernels: 72.6 us -> 63.9 us
    pallas_call x1, Pallas kernels: 60.1 us -> 53.9 us  [per_device(): pl.pallas_call(functools.partial(layer_kernel, dims), out_shape=(pltpu.VM...]
    pallas_call x1, Pallas kernels: 12.5 us -> 10.1 us  [per_device(): pl.pallas_call(functools.partial(gradient_kernel, dims, cells_all), grid=...]
where the time goes in v3:
time: 64.8 us; the launch traced here: 64.6 us
  Pallas kernels  63.9 us (99%)
  between operations  0.69 us (1%)
    pallas_call x1, Pallas kernels, per_device(): pl.pallas_call(functools.partial(layer_kernel, dims), out_shape=(pltpu.VM...  53.9 us
    pallas_call x1, Pallas kernels, per_device(): pl.pallas_call(functools.partial(gradient_kernel, dims, cells_all), grid=...  10.1 us

profile of v3, /device:TPU:0, one launch (start us, length us, event | category | flops | bytes accessed | tf_op | source)
XLA Modules:
  0.0 64.6 jit_solution(8555578821410135050)
XLA Ops:
  0.6 0.0 copy-start
  0.6 0.0 copy-start.1
  0.7 0.0 copy-start.2
  0.7 53.9 %layer.1 = (f32[1,4,32,64,256]{4,3,2,1,0:T(8,128)S(1)}, f32[256,128]{1,0:T(8,128)S(1)}, f32[256,128]{1,0:T(8,128)S(1)}, f32[4,256,128]{2,1,0:T(8,128)S(1)}) custom-call(f32[1,4,32,64,256]{4,3,2,1,0:T(8,128)} %f_hbm.1, f32[1,4,32,64,256]{4,3,2,1,0:T(8,128)} %g_hbm.1, f32[512,16,16]{2,1,0:T(8,128)} %bitcast.2, f32[4,4]{1,0:T(4,128)} %pw.1, f32[4]{0:T(128)} %bias.1, ...), custom_call_target="tpu_custom_call" | custom-call | tf_op jit(solution)/shard_map/layer/pallas_call | solution.py:515
  54.5 0.0 copy-done
  54.5 0.0 copy-done.1
  54.6 0.0 copy-done.2
  54.6 10.1 %gradients.1 = (f32[1,4,32,64,256]{4,3,2,1,0:T(8,128)}, f32[512,16,16]{2,1,0:T(8,128)}) custom-call(f32[256,128]{1,0:T(8,128)S(1)} %get-tuple-element.8.u_ref, f32[256,128]{1,0:T(8,128)S(1)} %get-tuple-element.9.h_ref, f32[4,256,128]{2,1,0:T(8,128)S(1)} %get-tuple-element.10.wd_ref, f32[256,130]{1,0:T(8,128)S(1)} %copy-done.1, ...), custom_call_target="tpu_custom_call" | custom-call | tf_op jit(solution)/shard_map/gradients/pallas_call | solution.py:545
Async XLA Ops:
  0.6 53.9 %copy-start = (bf16[512,1024]{1,0:T(8,128)(2,1)S(1)}, bf16[512,1024]{1,0:T(8,128)(2,1)}, u32[]{:S(2)}) copy-start(bf16[512,1024]{1,0:T(8,128)(2,1)} %constant.13.clone.sy_hbm.sy_ref) | copy-start | bytes 3145732
  0.6 53.9 %copy-start.1 = (f32[256,130]{1,0:T(8,128)S(1)}, f32[256,130]{1,0:T(8,128)}, u32[]{:S(2)}) copy-start(f32[256,130]{1,0:T(8,128)} %constant.14.clone.ph_ref) | copy-start | bytes 399364
  0.7 53.9 %copy-start.2 = (bf16[256,512]{1,0:T(8,128)(2,1)S(1)}, bf16[256,512]{1,0:T(8,128)(2,1)}, u32[]{:S(2)}) copy-start(bf16[256,512]{1,0:T(8,128)(2,1)} %constant.11.clone.l_hbm.l_ref) | copy-start | bytes 786436

commit v4 on v3

--- a/solution.py
+++ b/solution.py
@@ -15,6 +15,7 @@
 TILE = 512
 ROWS = 8
 LANES = 128
+HALF_ROOT = math.sqrt(0.5)
 
 
 def split(value):
@@ -36,7 +37,7 @@
 
 def x_tables(chans, length, modes, cells):
     angle = 2.0 * np.pi / length * ((np.arange(length)[:, None] * np.arange(modes)) % length)
-    weight = np.where(np.arange(modes) == 0, 1.0, 2.0) / cells
+    weight = np.where(np.arange(modes) == 0, 1.0, 2.0) / cells * HALF_ROOT
     first = np.stack([np.cos(angle), -np.sin(angle)], 1)
     eye = np.eye(chans).reshape(chans, chans // 2, 2)
     wide = np.einsum("cgd,xkp->cxgkdp", eye, first).reshape(chans, 1, length, -1)
@@ -139,10 +140,9 @@
     return dot(lhs[c // 2], l_v[:, c % 2 * nx : (c % 2 + 1) * nx])
 
 
-def gelu_slope(v):
-    arg = v * math.sqrt(0.5)
-    gauss = jnp.exp2(arg * arg * (-1.0 / math.log(2.0)))
-    return (0.5 * lax.erf(arg) + 0.5) + (v * (1.0 / math.sqrt(2.0 * math.pi))) * gauss
+def twice_gelu_slope(t):
+    gauss = jnp.exp2(t * t * (-1.0 / math.log(2.0)))
+    return (lax.erf(t) + 1.0) + (t * (2.0 / math.sqrt(math.pi))) * gauss
 
 
 def layer_kernel(dims, f_hbm, g_hbm, w_hbm, pw, bias, wt_hbm, l_hbm, an_hbm, sy_hbm, ph_ref,
@@ -277,9 +277,9 @@
         zs = pl.ds(pl.multiple_of(z * step, step), step)
         fields = [f_v[i, y, zs, :] for i in range(chans)]
         for o in range(chans):
-            total = fields[0] * pw[0, o] + bias[o]
+            total = fields[0] * (pw[0, o] * HALF_ROOT) + bias[o] * HALF_ROOT
             for i in range(1, chans):
-                total += fields[i] * pw[i, o]
+                total += fields[i] * (pw[i, o] * HALF_ROOT)
             loc_v[o, y, zs, :] = total
         return carry
 
@@ -315,7 +315,6 @@
         source = lane // (LANES // 2) * quarter + lane % quarter
         mg[pl.ds(me, 1)] = jnp.where(is_real, take(real, source), take(imag, source))[None]
         gather_start(mg, sm, rm)
-        gather_start(ug, su, ru)
 
     owner(mix_first)
 
@@ -329,6 +328,7 @@
     sy_copy.wait()
     l_copy.wait()
     gather_wait(mg, sm, rm)
+    owner(lambda: gather_start(ug, su, ru))
 
     def load_turn(ref):
         m = ref[...].reshape(modes, LANES)
@@ -348,7 +348,7 @@
         pairs = 0.0
         for o in range(chans):
             pre = back_to_x(lhs, l_v, o) + loc_v[o, lines].reshape(tile, nx)
-            up = g_v[o, lines].reshape(tile, nx) * gelu_slope(pre)
+            up = g_v[o, lines].reshape(tile, nx) * twice_gelu_slope(pre)
             g_v[o, lines] = up.reshape(ty, zlines, nx)
             pairs += along_x(up, o, xs, wt_v)
         analyse(pairs, an_v, acc, step_cos, step_sin)
@@ -364,9 +364,9 @@
             zs = pl.ds(pl.multiple_of(z * step, step), step)
             ups = [g_v[o, y, zs, :] for o in range(chans)]
             for i in range(chans):
-                total = ups[0] * pw[i, 0]
+                total = ups[0] * (pw[i, 0] * 0.5)
                 for o in range(1, chans):
-                    total += ups[o] * pw[i, o]
+                    total += ups[o] * (pw[i, o] * 0.5)
                 loc_v[i, y, zs, :] = total
             return carry
 
@@ -376,7 +376,7 @@
     lax.fori_loop(0, steps, back, 0)
 
     def last():
-        hg[pl.ds(me, 1)] = scatter_sum(part.at[1], got2, s2, r2)[None]
+        hg[pl.ds(me, 1)] = 0.5 * scatter_sum(part.at[1], got2, s2, r2)[None]
         gather_start(hg, sh, rh)
 
     owner(last)
@@ -434,7 +434,7 @@
             column = jnp.sum(jnp.where(place, ph_ref[:, k * count : (k + 1) * count], 0.0), axis=1, keepdims=True)
             found.append(jnp.broadcast_to(column, (modes, LANES)))
             phase[k] = jnp.broadcast_to(ph_ref[:, 4 * count + k : 4 * count + k + 1], (modes, LANES))
-        m = adjoint(h_ref[...], [wd_ref[b] for b in range(chans)], chans, mx)
+        m = adjoint(h_ref[...], [wd_ref[b] for b in range(chans)], chans, mx) * (1.0 / HALF_ROOT)
         im = times_i(m)
         turn[0] = m * found[0] + im * found[1]
         turn[1] = im * found[0] - m * found[1]

time: 64.8 us -> 63.3 us (0.977)
  Pallas kernels: 63.9 us -> 62.4 us
    pallas_call x1, Pallas kernels: 53.9 us -> 52.4 us  [per_device(): pl.pallas_call(functools.partial(layer_kernel, dims), out_shape=(pltpu.VM...]
where the time goes in v4:
time: 63.3 us; the launch traced here: 63.1 us
  Pallas kernels  62.4 us (99%)
  between operations  0.69 us (1%)
    pallas_call x1, Pallas kernels, per_device(): pl.pallas_call(functools.partial(layer_kernel, dims), out_shape=(pltpu.VM...  52.4 us
    pallas_call x1, Pallas kernels, per_device(): pl.pallas_call(functools.partial(gradient_kernel, dims, cells_all), grid=...  10.1 us

profile of v4, /device:TPU:0, one launch (start us, length us, event | category | flops | bytes accessed | tf_op | source)
XLA Modules:
  0.0 63.1 jit_solution(11979880672129435164)
XLA Ops:
  0.6 0.0 copy-start
  0.6 0.0 copy-start.1
  0.7 0.0 copy-start.2
  0.7 52.4 %layer.1 = (f32[1,4,32,64,256]{4,3,2,1,0:T(8,128)S(1)}, f32[256,128]{1,0:T(8,128)S(1)}, f32[256,128]{1,0:T(8,128)S(1)}, f32[4,256,128]{2,1,0:T(8,128)S(1)}) custom-call(f32[1,4,32,64,256]{4,3,2,1,0:T(8,128)} %f_hbm.1, f32[1,4,32,64,256]{4,3,2,1,0:T(8,128)} %g_hbm.1, f32[512,16,16]{2,1,0:T(8,128)} %bitcast.2, f32[4,4]{1,0:T(4,128)} %pw.1, f32[4]{0:T(128)} %bias.1, ...), custom_call_target="tpu_custom_call" | custom-call | tf_op jit(solution)/shard_map/layer/pallas_call | solution.py:515
  53.0 0.0 copy-done
  53.0 0.0 copy-done.1
  53.0 0.0 copy-done.2
  53.1 10.1 %gradients.1 = (f32[1,4,32,64,256]{4,3,2,1,0:T(8,128)}, f32[512,16,16]{2,1,0:T(8,128)}) custom-call(f32[256,128]{1,0:T(8,128)S(1)} %get-tuple-element.8.u_ref, f32[256,128]{1,0:T(8,128)S(1)} %get-tuple-element.9.h_ref, f32[4,256,128]{2,1,0:T(8,128)S(1)} %get-tuple-element.10.wd_ref, f32[256,130]{1,0:T(8,128)S(1)} %copy-done.1, ...), custom_call_target="tpu_custom_call" | custom-call | tf_op jit(solution)/shard_map/gradients/pallas_call | solution.py:545
Async XLA Ops:
  0.6 52.4 %copy-start = (bf16[512,1024]{1,0:T(8,128)(2,1)S(1)}, bf16[512,1024]{1,0:T(8,128)(2,1)}, u32[]{:S(2)}) copy-start(bf16[512,1024]{1,0:T(8,128)(2,1)} %constant.13.clone.sy_hbm.sy_ref) | copy-start | bytes 3145732
  0.6 52.4 %copy-start.1 = (f32[256,130]{1,0:T(8,128)S(1)}, f32[256,130]{1,0:T(8,128)}, u32[]{:S(2)}) copy-start(f32[256,130]{1,0:T(8,128)} %constant.14.clone.ph_ref) | copy-start | bytes 399364
  0.7 52.4 %copy-start.2 = (bf16[256,512]{1,0:T(8,128)(2,1)S(1)}, bf16[256,512]{1,0:T(8,128)(2,1)}, u32[]{:S(2)}) copy-start(bf16[256,512]{1,0:T(8,128)(2,1)} %constant.11.clone.l_hbm.l_ref) | copy-start | bytes 786436

commit v5 on v4

--- a/solution.py
+++ b/solution.py
@@ -80,13 +80,12 @@
     return jnp.where(real, -pltpu.roll(value, LANES - quarter, 1), pltpu.roll(value, quarter, 1))
 
 
-def along_x(value, c, xs, wt_v):
+def keep_split(value, c, xs):
     width = value.shape[1]
     at = 2 * c * width
     high, low = split(value)
     xs[:, at : at + width] = high
     xs[:, at + width : at + 2 * width] = low
-    return dot(xs[:, at : at + 2 * width], wt_v[at : at + 2 * width, :])
 
 
 def analyse(pairs, an_v, acc, step_cos, step_sin):
@@ -207,10 +206,9 @@
     def first(j, carry):
         tile_copy(f_hbm, f_v, f_sem, j).wait()
 
-        pairs = 0.0
         for c in range(chans):
-            pairs += along_x(f_v[c, pl.ds(j * ty, ty)].reshape(tile, nx), c, xs, wt_v)
-        analyse(pairs, an_v, acc, step_cos, step_sin)
+            keep_split(f_v[c, pl.ds(j * ty, ty)].reshape(tile, nx), c, xs)
+        analyse(dot(xs[...], wt_v[...]), an_v, acc, step_cos, step_sin)
         return carry
 
     lax.fori_loop(0, steps, first, 0)
@@ -345,13 +343,12 @@
         turn_on(turn, step_cos, step_sin)
         tile_copy(g_hbm, g_v, g_sem, j).wait()
         lines = pl.ds(j * ty, ty)
-        pairs = 0.0
         for o in range(chans):
             pre = back_to_x(lhs, l_v, o) + loc_v[o, lines].reshape(tile, nx)
             up = g_v[o, lines].reshape(tile, nx) * twice_gelu_slope(pre)
             g_v[o, lines] = up.reshape(ty, zlines, nx)
-            pairs += along_x(up, o, xs, wt_v)
-        analyse(pairs, an_v, acc, step_cos, step_sin)
+            keep_split(up, o, xs)
+        analyse(dot(xs[...], wt_v[...]), an_v, acc, step_cos, step_sin)
         return carry
 
     lax.fori_loop(0, steps, second, 0)

time: 63.3 us -> 61.9 us (0.978)
  Pallas kernels: 62.4 us -> 61.1 us
    pallas_call x1, Pallas kernels: 52.4 us -> 51 us  [per_device(): pl.pallas_call(functools.partial(layer_kernel, dims), out_shape=(pltpu.VM...]
where the time goes in v5:
time: 61.9 us; the launch traced here: 61.8 us
  Pallas kernels  61.1 us (99%)
  between operations  0.69 us (1%)
    pallas_call x1, Pallas kernels, per_device(): pl.pallas_call(functools.partial(layer_kernel, dims), out_shape=(pltpu.VM...  51 us
    pallas_call x1, Pallas kernels, per_device(): pl.pallas_call(functools.partial(gradient_kernel, dims, cells_all), grid=...  10.1 us

profile of v5, /device:TPU:0, one launch (start us, length us, event | category | flops | bytes accessed | tf_op | source)
XLA Modules:
  0.0 61.8 jit_solution(7779837889357920442)
XLA Ops:
  0.6 0.0 copy-start
  0.6 0.0 copy-start.1
  0.7 0.0 copy-start.2
  0.7 51.0 %layer.1 = (f32[1,4,32,64,256]{4,3,2,1,0:T(8,128)S(1)}, f32[256,128]{1,0:T(8,128)S(1)}, f32[256,128]{1,0:T(8,128)S(1)}, f32[4,256,128]{2,1,0:T(8,128)S(1)}) custom-call(f32[1,4,32,64,256]{4,3,2,1,0:T(8,128)} %f_hbm.1, f32[1,4,32,64,256]{4,3,2,1,0:T(8,128)} %g_hbm.1, f32[512,16,16]{2,1,0:T(8,128)} %bitcast.2, f32[4,4]{1,0:T(4,128)} %pw.1, f32[4]{0:T(128)} %bias.1, ...), custom_call_target="tpu_custom_call" | custom-call | tf_op jit(solution)/shard_map/layer/pallas_call | solution.py:512
  51.7 0.0 copy-done
  51.7 0.0 copy-done.1
  51.7 0.0 copy-done.2
  51.7 10.1 %gradients.1 = (f32[1,4,32,64,256]{4,3,2,1,0:T(8,128)}, f32[512,16,16]{2,1,0:T(8,128)}) custom-call(f32[256,128]{1,0:T(8,128)S(1)} %get-tuple-element.8.u_ref, f32[256,128]{1,0:T(8,128)S(1)} %get-tuple-element.9.h_ref, f32[4,256,128]{2,1,0:T(8,128)S(1)} %get-tuple-element.10.wd_ref, f32[256,130]{1,0:T(8,128)S(1)} %copy-done.1, ...), custom_call_target="tpu_custom_call" | custom-call | tf_op jit(solution)/shard_map/gradients/pallas_call | solution.py:542
Async XLA Ops:
  0.6 51.1 %copy-start = (bf16[512,1024]{1,0:T(8,128)(2,1)S(1)}, bf16[512,1024]{1,0:T(8,128)(2,1)}, u32[]{:S(2)}) copy-start(bf16[512,1024]{1,0:T(8,128)(2,1)} %constant.13.clone.sy_hbm.sy_ref) | copy-start | bytes 3145732
  0.6 51.1 %copy-start.1 = (f32[256,130]{1,0:T(8,128)S(1)}, f32[256,130]{1,0:T(8,128)}, u32[]{:S(2)}) copy-start(f32[256,130]{1,0:T(8,128)} %constant.14.clone.ph_ref) | copy-start | bytes 399364
  0.7 51.1 %copy-start.2 = (bf16[256,512]{1,0:T(8,128)(2,1)S(1)}, bf16[256,512]{1,0:T(8,128)(2,1)}, u32[]{:S(2)}) copy-start(bf16[256,512]{1,0:T(8,128)(2,1)} %constant.11.clone.l_hbm.l_ref) | copy-start | bytes 786436
